TPU v7x, 16 devices: a whole 2x2x2 slice. The times are simulated.
16 devices in a mesh: tp: 2 (over z), fsdp: 8 (over y, x, core).
Axes of the slice: x: 2, y: 2, z: 2, core: 2. Of those that a mesh axis runs over, the one named last changes fastest.
Arguments:
- patches: bfloat16 [256, 49, 3072], P('fsdp')
- labels: int32 [256], P('fsdp')
- w_stem: float32 [3072, 512], P('fsdp', 'tp')
- b_stem: float32 [512], P(('tp', 'fsdp'))
- ln1_g: float32 [2, 512], P(None, ('tp', 'fsdp'))
- ln1_b: float32 [2, 512], P(None, ('tp', 'fsdp'))
- w_tok1: float32 [2, 49, 256], P(None, None, 'fsdp')
- b_tok1: float32 [2, 256], P(None, 'fsdp')
- w_tok2: float32 [2, 256, 49], P(None, 'fsdp')
- ln2_g: float32 [2, 512], P(None, ('tp', 'fsdp'))
- ln2_b: float32 [2, 512], P(None, ('tp', 'fsdp'))
- w_ch1: float32 [2, 512, 2048], P(None, 'fsdp', 'tp')
- b_ch1: float32 [2, 2048], P(None, ('tp', 'fsdp'))
- w_ch2: float32 [2, 2048, 512], P(None, ('tp', 'fsdp'))
- b_ch2: float32 [2, 512], P(None, ('tp', 'fsdp'))
- lnf_g: float32 [512], P(('tp', 'fsdp'))
- lnf_b: float32 [512], P(('tp', 'fsdp'))
- w_head: float32 [512, 1000], P('fsdp', 'tp')
- b_head: float32 [1000], P('tp')
Outputs:
- output 1: float32 [], replicated
- output 2: float32 [3072, 512], P('fsdp', 'tp')
- output 3: float32 [512], P(('tp', 'fsdp'))
- output 4: float32 [2, 512], P(None, ('tp', 'fsdp'))
- output 5: float32 [2, 512], P(None, ('tp', 'fsdp'))
- output 6: float32 [2, 49, 256], P(None, None, 'fsdp')
- output 7: float32 [2, 256], P(None, 'fsdp')
- output 8: float32 [2, 256, 49], P(None, 'fsdp')
- output 9: float32 [2, 512], P(None, ('tp', 'fsdp'))
- output 10: float32 [2, 512], P(None, ('tp', 'fsdp'))
- output 11: float32 [2, 512, 2048], P(None, 'fsdp', 'tp')
- output 12: float32 [2, 2048], P(None, ('tp', 'fsdp'))
- output 13: float32 [2, 2048, 512], P(None, ('tp', 'fsdp'))
- output 14: float32 [2, 512], P(None, ('tp', 'fsdp'))
- output 15: float32 [512], P(('tp', 'fsdp'))
- output 16: float32 [512], P(('tp', 'fsdp'))
- output 17: float32 [512, 1000], P('fsdp', 'tp')
- output 18: float32 [1000], P('tp')
All inputs are finite; a program needn't handle non-finite values.
Results may differ from a plain program's by a relative error of at most 0.0151881.
Values are sent between devices in bfloat16 or wider.
A program may use at most 1 GiB of HBM per device.

v0:
```python
import jax
import jax.numpy as jnp
from jax import lax
from jax.sharding import PartitionSpec as P

EPS = 1e-6
CHANNEL_AXES = ('tp', 'fsdp')
LAYER_NAMES = ('ln1_g', 'ln1_b', 'w_tok1', 'b_tok1', 'w_tok2', 'ln2_g', 'ln2_b', 'w_ch1', 'b_ch1', 'w_ch2', 'b_ch2')


def product(form, left, right):
    return jnp.einsum(form, left, right, preferred_element_type=jnp.float32)


def gather_weight(weight, axis):
    return lax.all_gather(weight.astype(jnp.bfloat16), 'fsdp', axis=axis, tiled=True)


def gather_vector(values):
    return lax.all_gather(values, 'fsdp', axis=values.ndim - 1, tiled=True)


def sum_to_piece(grad_full, axis):
    return lax.psum_scatter(grad_full, 'fsdp', scatter_dimension=axis, tiled=True)


def lead_sum(values):
    return jnp.sum(values.reshape(-1, values.shape[-1]), axis=0)


def norm_forward(values, gain, shift, width):
    moments = jnp.concatenate([jnp.sum(values, axis=-1, keepdims=True),
                               jnp.sum(values * values, axis=-1, keepdims=True)], axis=-1)
    moments = lax.psum(moments, 'tp') / width
    mean_val = moments[..., :1]
    inv_std = lax.rsqrt(jnp.maximum(moments[..., 1:] - mean_val * mean_val, 0.0) + EPS)
    standard = (values - mean_val) * inv_std
    return standard * gain + shift, standard, inv_std


def norm_backward(grad_out, gain, standard, inv_std, width):
    grad_std = grad_out * gain
    moments = jnp.concatenate([jnp.sum(grad_std, axis=-1, keepdims=True),
                               jnp.sum(grad_std * standard, axis=-1, keepdims=True)], axis=-1)
    moments = lax.psum(moments, 'tp') / width
    return inv_std * (grad_std - moments[..., :1] - standard * moments[..., 1:])


def gelu_grad(pre_act, grad_out):
    return jax.vjp(jax.nn.gelu, pre_act)[1](grad_out)[0]


def weight_specs():
    vec_spec = P(CHANNEL_AXES)
    layer_vec = P(None, CHANNEL_AXES)
    return (P('fsdp', 'tp'), vec_spec, layer_vec, layer_vec, P(None, None, 'fsdp'), P(None, 'fsdp'),
            P(None, 'fsdp', None), layer_vec, layer_vec, P(None, 'fsdp', 'tp'), layer_vec,
            P(None, CHANNEL_AXES, None), layer_vec, vec_spec, vec_spec, P('fsdp', 'tp'), P('tp'))


def solution(mesh):
    fsdp_size = mesh.shape['fsdp']
    tp_size = mesh.shape['tp']

    def step(patches, labels, w_stem, b_stem, ln1_g, ln1_b, w_tok1, b_tok1, w_tok2,
             ln2_g, ln2_b, w_ch1, b_ch1, w_ch2, b_ch2, lnf_g, lnf_b, w_head, b_head):
        local_images = patches.shape[0]
        tokens = patches.shape[1]
        channels = w_stem.shape[1] * tp_size
        total_images = local_images * fsdp_size
        stem_bias = gather_vector(b_stem)
        ln1_gain = gather_vector(ln1_g)
        ln1_shift = gather_vector(ln1_b)
        tok_bias = gather_vector(b_tok1)
        ln2_gain = gather_vector(ln2_g)
        ln2_shift = gather_vector(ln2_b)
        ch_bias1 = gather_vector(b_ch1)
        ch_bias2 = gather_vector(b_ch2)
        lnf_gain = gather_vector(lnf_g)
        lnf_shift = gather_vector(lnf_b)

        resid = product('bsp,pc->bsc', patches, gather_weight(w_stem, 0)) + stem_bias
        saved = []
        for layer in range(w_tok1.shape[0]):
            normed, norm1_std, norm1_inv = norm_forward(resid, ln1_gain[layer], ln1_shift[layer], channels)
            normed = normed.astype(jnp.bfloat16)
            tok_pre = product('bsc,sj->bcj', normed, gather_weight(w_tok1[layer], 1)) + tok_bias[layer]
            tok_act = jax.nn.gelu(tok_pre).astype(jnp.bfloat16)
            resid = resid + product('bcj,js->bsc', tok_act, gather_weight(w_tok2[layer], 0))
            normed2, norm2_std, norm2_inv = norm_forward(resid, ln2_gain[layer], ln2_shift[layer], channels)
            full_in = lax.all_gather(normed2.astype(jnp.bfloat16), 'tp', axis=2, tiled=True)
            ch_pre = product('bsc,cd->bsd', full_in, gather_weight(w_ch1[layer], 0)) + ch_bias1[layer]
            ch_act = jax.nn.gelu(ch_pre).astype(jnp.bfloat16)
            part_sum = product('bsd,dc->bsc', ch_act, gather_weight(w_ch2[layer], 0))
            resid = resid + lax.psum_scatter(part_sum, 'tp', scatter_dimension=2, tiled=True) + ch_bias2[layer]
            saved.append(dict(normed=normed, norm1_std=norm1_std, norm1_inv=norm1_inv, tok_pre=tok_pre,
                              tok_act=tok_act, norm2_std=norm2_std, norm2_inv=norm2_inv,
                              full_in=full_in, ch_pre=ch_pre, ch_act=ch_act))

        pooled = jnp.mean(resid, axis=1)
        head_in, head_std, head_inv = norm_forward(pooled, lnf_gain, lnf_shift, channels)
        head_full = lax.all_gather(head_in.astype(jnp.bfloat16), 'tp', axis=1, tiled=True)
        head_w = gather_weight(w_head, 0)
        logits = product('bc,ck->bk', head_full, head_w) + b_head
        class_local = logits.shape[1]
        class_ids = lax.axis_index('tp') * class_local + jnp.arange(class_local)
        is_label = class_ids[None, :] == labels[:, None]
        row_max = lax.pmax(jnp.max(logits, axis=1), 'tp')
        shifted = jnp.exp(logits - row_max[:, None])
        class_sums = lax.psum(jnp.stack([jnp.sum(shifted, axis=1),
                                         jnp.sum(jnp.where(is_label, logits, 0.0), axis=1)]), 'tp')
        log_norm = row_max + jnp.log(class_sums[0])
        loss = lax.psum(jnp.sum(log_norm - class_sums[1]), 'fsdp') / total_images

        d_logits = (shifted / class_sums[0][:, None] - is_label.astype(jnp.float32)) / total_images
        d_logits_bf = d_logits.astype(jnp.bfloat16)
        g_w_head = sum_to_piece(product('bc,bk->ck', head_full, d_logits_bf), 0)
        g_b_head = lax.psum(jnp.sum(d_logits, axis=0), 'fsdp')
        d_head_in = lax.psum_scatter(product('bk,ck->bc', d_logits_bf, head_w), 'tp', scatter_dimension=1, tiled=True)
        g_lnf_g = sum_to_piece(jnp.sum(d_head_in * head_std, axis=0), 0)
        g_lnf_b = sum_to_piece(jnp.sum(d_head_in, axis=0), 0)
        d_pooled = norm_backward(d_head_in, lnf_gain, head_std, head_inv, channels)
        d_resid = jnp.broadcast_to((d_pooled / tokens)[:, None, :], resid.shape)

        grad_lists = {name: [] for name in LAYER_NAMES}
        for layer in reversed(range(w_tok1.shape[0])):
            keep = saved[layer]
            grad_lists['b_ch2'].append(sum_to_piece(lead_sum(d_resid), 0))
            d_out_full = lax.all_gather(d_resid.astype(jnp.bfloat16), 'tp', axis=2, tiled=True)
            ch_w1 = gather_weight(w_ch1[layer], 0)
            ch_w2 = gather_weight(w_ch2[layer], 0)
            grad_lists['w_ch2'].append(sum_to_piece(product('bsd,bsc->dc', keep['ch_act'], d_out_full), 0))
            d_ch_pre = gelu_grad(keep['ch_pre'], product('bsc,dc->bsd', d_out_full, ch_w2))
            grad_lists['b_ch1'].append(sum_to_piece(lead_sum(d_ch_pre), 0))
            d_ch_pre_bf = d_ch_pre.astype(jnp.bfloat16)
            grad_lists['w_ch1'].append(sum_to_piece(product('bsc,bsd->cd', keep['full_in'], d_ch_pre_bf), 0))
            d_norm2 = lax.psum_scatter(product('bsd,cd->bsc', d_ch_pre_bf, ch_w1), 'tp', scatter_dimension=2, tiled=True)
            grad_lists['ln2_g'].append(sum_to_piece(lead_sum(d_norm2 * keep['norm2_std']), 0))
            grad_lists['ln2_b'].append(sum_to_piece(lead_sum(d_norm2), 0))
            d_mid = d_resid + norm_backward(d_norm2, ln2_gain[layer], keep['norm2_std'], keep['norm2_inv'], channels)
            d_mid_bf = d_mid.astype(jnp.bfloat16)
            tok_w1 = gather_weight(w_tok1[layer], 1)
            tok_w2 = gather_weight(w_tok2[layer], 0)
            grad_lists['w_tok2'].append(lax.psum(sum_to_piece(product('bcj,bsc->js', keep['tok_act'], d_mid_bf), 0), 'tp'))
            d_tok_pre = gelu_grad(keep['tok_pre'], product('bsc,js->bcj', d_mid_bf, tok_w2))
            grad_lists['b_tok1'].append(lax.psum(sum_to_piece(lead_sum(d_tok_pre), 0), 'tp'))
            d_tok_pre_bf = d_tok_pre.astype(jnp.bfloat16)
            grad_lists['w_tok1'].append(lax.psum(sum_to_piece(product('bsc,bcj->sj', keep['normed'], d_tok_pre_bf), 1), 'tp'))
            d_norm1 = product('bcj,sj->bsc', d_tok_pre_bf, tok_w1)
            grad_lists['ln1_g'].append(sum_to_piece(lead_sum(d_norm1 * keep['norm1_std']), 0))
            grad_lists['ln1_b'].append(sum_to_piece(lead_sum(d_norm1), 0))
            d_resid = d_mid + norm_backward(d_norm1, ln1_gain[layer], keep['norm1_std'], keep['norm1_inv'], channels)

        g_b_stem = sum_to_piece(lead_sum(d_resid), 0)
        g_w_stem = sum_to_piece(product('bsp,bsc->pc', patches, d_resid.astype(jnp.bfloat16)), 0)
        stacked = [jnp.stack(grad_lists[name][::-1]) for name in LAYER_NAMES]
        return tuple([loss, g_w_stem, g_b_stem] + stacked + [g_lnf_g, g_lnf_b, g_w_head, g_b_head])

    specs = weight_specs()
    return jax.shard_map(step, mesh=mesh, in_specs=(P('fsdp', None, None), P('fsdp')) + specs,
                         out_specs=(P(),) + specs, check_vma=False)
```

profile of v0, /device:TPU:0, one launch (start us, length us, event | category | flops | bytes accessed | tf_op | source)
XLA Modules:
  0.0 952.4 jit_solution(17049996691853507030)
XLA Ops:
  10.9 10.7 %all-gather.10 = f32[8,32,2]{1,2,0:T(2,128)S(1)} all-gather(f32[1,32,2]{1,2,0:T(2,128)} %bitcast.369), channel_id=1, replica_groups=mesh['tp'=2,'fsdp'=8] {'fsdp'}, dimensions={0}, use_global_device_ids=true | all-gather | bytes 2304 | tf_op jit(solution)/shard_map/all_gather | solution.py:20
  80.0 13.7 %all-reduce.21 = (f32[256]{0:T(256)}, f32[256]{0:T(256)}, f32[256]{0:T(256)S(1)}) all-reduce(f32[256]{0:T(256)S(1)} %dynamic-update-slice.2, f32[256]{0:T(256)S(1)} %dynamic-update-slice.1, f32[256]{0:T(256)S(1)} %dynamic-update-slice), channel_id=1, replica_groups=mesh['tp'=2,'fsdp'=8] {'fsdp'}, use_global_device_ids=true, to_apply=%add.2 | all-reduce | flops 768 | bytes 6144
  138.7 14.6 %all-gather.25.cloned.1.call-done = bf16[32,49,512]{2,0,1:T(8,128)(2,1)} async-done(((bf16[32,49,256]{2,0,1:T(8,128)(2,1)}), bf16[32,49,512]{2,0,1:T(8,128)(2,1)}) %all-gather.25.cloned.1.call-update) | async-done | bytes 1605648 | tf_op jit(solution)/shard_map/all_gather | solution.py:91
  163.2 11.8 %all-gather.33.cloned.1.call-done = bf16[1,1024,512]{2,1,0:T(8,128)(2,1)} async-done(((bf16[1,128,512]{2,1,0:T(8,128)(2,1)}), bf16[1,1024,512]{2,1,0:T(8,128)(2,1)}) %all-gather.33.cloned.1.call-update) | async-done | bytes 1048592 | tf_op jit(solution)/shard_map/all_gather | solution.py:16
  208.9 15.0 %reduce-scatter.16.cloned.1.call-done = f32[32,49,256]{2,0,1:T(8,128)} async-done(((f32[32,49,512]{2,0,1:T(8,128)}), f32[32,49,256]{2,0,1:T(8,128)}) %reduce-scatter.16.cloned.1.call-update) | async-done | bytes 1605648 | tf_op jit(solution)/shard_map/reduce_scatter | solution.py:95
  255.6 24.7 %all-gather.27.cloned.1.call-done = bf16[32,49,512]{2,0,1:T(8,128)(2,1)} async-done(((bf16[32,49,256]{2,0,1:T(8,128)(2,1)}), bf16[32,49,512]{2,0,1:T(8,128)(2,1)}) %all-gather.27.cloned.1.call-update) | async-done | bytes 1605648 | tf_op jit(solution)/shard_map/all_gather | solution.py:91
  290.3 11.8 %all-gather.37.cloned.1.call-done = bf16[1,1024,512]{2,1,0:T(8,128)(2,1)} async-done(((bf16[1,128,512]{2,1,0:T(8,128)(2,1)}), bf16[1,1024,512]{2,1,0:T(8,128)(2,1)}) %all-gather.37.cloned.1.call-update) | async-done | bytes 1048592 | tf_op jit(solution)/shard_map/all_gather | solution.py:16
  309.7 10.2 %all_gather.105 = bf16[512,500]{1,0:T(8,128)(2,1)} all-gather(bf16[64,500]{1,0:T(8,128)(2,1)S(1)} %convert_element_type.125), channel_id=1, replica_groups=mesh['tp'=2,'fsdp'=8] {'fsdp'}, dimensions={0}, use_global_device_ids=true | all-gather | bytes 576000 | tf_op jit(solution)/shard_map/all_gather | solution.py:16
  319.9 31.1 %reduce-scatter.18.cloned.1.call-done = f32[32,49,256]{2,0,1:T(8,128)} async-done(((f32[32,49,512]{2,0,1:T(8,128)}), f32[32,49,256]{2,0,1:T(8,128)}) %reduce-scatter.18.cloned.1.call-update) | async-done | bytes 1605648 | tf_op jit(solution)/shard_map/reduce_scatter | solution.py:95
  412.4 42.3 %reduce-scatter.22.cloned.1.call-done = f32[32,49,256]{2,0,1:T(8,128)} async-done(((f32[32,49,512]{2,0,1:T(8,128)}), f32[32,49,256]{2,0,1:T(8,128)}) %reduce-scatter.22.cloned.1.call-update) | async-done | bytes 1605648 | tf_op jit(solution)/shard_map/reduce_scatter | solution.py:137
  470.0 10.3 %fusion.160 = (f32[256]{0:T(256)}, bf16[32,256,256]{2,1,0:T(8,128)(2,1)S(1)}) fusion(f32[32,256,256]{2,1,0:T(8,128)} %get-tuple-element.196, f32[256]{0:T(256)S(1)} %bitcast.378, bf16[1,256,49]{2,1,0:T(8,128)(2,1)} %copy-done.33, bf16[32,49,256]{2,0,1:T(8,128)(2,1)S(1)} %fusion.96), kind=kOutput, calls=%fused_computation.276 | convolution fusion | flops 251657984 | bytes 13412864 | tf_op jit(solution)/shard_map/bsc,js->bcj/dot_general | solution.py:12
  485.1 10.2 %psum.142 = f32[32,49,2]{0,1,2:T(8,128)} all-reduce(f32[32,49,2]{0,1,2:T(8,128)} %pad_maximum_fusion.7), channel_id=1, replica_groups=mesh['tp'=2,'fsdp'=8] {'tp'}, use_global_device_ids=true, to_apply=%region_35.36 | all-reduce | flops 3136 | bytes 25088 | tf_op jit(solution)/shard_map/psum | solution.py:45
  503.4 25.4 %all-gather.29.cloned.1.call-done = bf16[32,49,512]{2,0,1:T(8,128)(2,1)} async-done(((bf16[32,49,256]{2,0,1:T(8,128)(2,1)}), bf16[32,49,512]{2,0,1:T(8,128)(2,1)}) %all-gather.29.cloned.1.call-update) | async-done | bytes 1605648 | tf_op jit(solution)/shard_map/all_gather | solution.py:129
  528.8 11.3 %fusion.143 = (f32[1024]{0:T(1024)}, bf16[32,49,1024]{2,1,0:T(8,128)(2,1)S(1)}) fusion(f32[32,49,1024]{2,1,0:T(8,128)} %get-tuple-element.194, f32[1024]{0:T(1024)S(1)} %bitcast.359, bf16[1,1024,512]{2,1,0:T(8,128)(2,1)S(1)} %copy-done.75, bf16[32,49,512]{2,0,1:T(8,128)(2,1)} %all-gather.29.cloned.1.call-done), kind=kOutput, calls=%fused_computation.259 | convolution fusion | flops 1679490048 | bytes 12296192 | tf_op jit(solution)/shard_map/bsc,dc->bsd/dot_general | solution.py:12
  602.2 10.3 %fusion.161 = (f32[256]{0:T(256)}, bf16[32,256,256]{2,1,0:T(8,128)(2,1)S(1)}) fusion(f32[32,256,256]{2,1,0:T(8,128)} %get-tuple-element.192, f32[256]{0:T(256)S(1)} %bitcast.376, bf16[1,256,49]{2,1,0:T(8,128)(2,1)S(1)} %copy-done.30, bf16[32,49,256]{2,0,1:T(8,128)(2,1)S(1)} %get-tuple-element.134), kind=kOutput, calls=%fused_computation.277 | convolution fusion | flops 251657984 | bytes 13412864 | tf_op jit(solution)/shard_map/bsc,js->bcj/dot_general | solution.py:12
  652.6 13.1 %reduce-scatter.36.cloned.1.call-done = f32[64,1024]{1,0:T(8,128)} async-done(((f32[512,1024]{1,0:T(8,128)}), f32[64,1024]{1,0:T(8,128)}) %reduce-scatter.36.cloned.1.call-update) | async-done | bytes 262160 | tf_op jit(solution)/shard_map/reduce_scatter | solution.py:24
  667.5 36.6 %reduce-scatter.42.cloned.1.call-done = f32[128,512]{1,0:T(8,128)} async-done(((f32[1024,512]{1,0:T(8,128)}), f32[128,512]{1,0:T(8,128)}) %reduce-scatter.42.cloned.1.call-update) | async-done | bytes 262160 | tf_op jit(solution)/shard_map/reduce_scatter | solution.py:24
  704.1 38.4 %reduce-scatter.40.cloned.1.call-done = f32[128,512]{1,0:T(8,128)} async-done(((f32[1024,512]{1,0:T(8,128)}), f32[128,512]{1,0:T(8,128)}) %reduce-scatter.40.cloned.1.call-update) | async-done | bytes 262160 | tf_op jit(solution)/shard_map/reduce_scatter | solution.py:24
  744.5 23.4 %all-reduce.20 = (f32[]{:T(128)}, f32[256]{0:T(256)S(1)}, f32[256]{0:T(256)S(1)}, f32[256]{0:T(256)S(1)}, f32[256]{0:T(256)S(1)}, /*index=5*/f32[256]{0:T(256)S(...) all-reduce(f32[]{:T(128)} %fusion.131, ...), channel_id=1, replica_groups=mesh['tp'=2,'fsdp'=8] {'fsdp'}, use_global_device_ids=true, to_apply=%region_24.25 | all-reduce | flops 6389 | bytes 51112 | tf_op jit(solution)/shard_map/psum | solution.py:113
  774.3 30.7 %reduce-scatter.34.cloned.1.call-done = f32[32,49]{1,0:T(8,128)} async-done(((f32[256,49]{1,0:T(8,128)}), f32[32,49]{1,0:T(8,128)}) %reduce-scatter.34.cloned.1.call-update) | async-done | bytes 6288 | tf_op jit(solution)/shard_map/reduce_scatter | solution.py:24
  805.0 30.8 %reduce-scatter.28.cloned.1.call-done = f32[49,32]{0,1:T(8,128)} async-done(((f32[49,256]{0,1:T(8,128)}), f32[49,32]{0,1:T(8,128)}) %reduce-scatter.28.cloned.1.call-update) | async-done | bytes 6288 | tf_op jit(solution)/shard_map/reduce_scatter | solution.py:24
  835.7 30.9 %reduce-scatter.32.cloned.1.call-done = f32[32,49]{1,0:T(8,128)} async-done(((f32[256,49]{1,0:T(8,128)}), f32[32,49]{1,0:T(8,128)}) %reduce-scatter.32.cloned.1.call-update) | async-done | bytes 6288 | tf_op jit(solution)/shard_map/reduce_scatter | solution.py:24
  878.3 31.9 %reduce-scatter.26.cloned.1.call-done = f32[384,256]{0,1:T(8,128)} async-done(((f32[3072,256]{0,1:T(8,128)}), f32[384,256]{0,1:T(8,128)}) %reduce-scatter.26.cloned.1.call-update) | async-done | bytes 393232 | tf_op jit(solution)/shard_map/reduce_scatter | solution.py:24
  912.2 32.1 %reduce-scatter.44.cloned.1.call-done = f32[64,500]{1,0:T(8,128)} async-done(((f32[512,500]{1,0:T(8,128)}), f32[64,500]{1,0:T(8,128)}) %reduce-scatter.44.cloned.1.call-update) | async-done | bytes 128016 | tf_op jit(solution)/shard_map/reduce_scatter | solution.py:24
  (372 shorter events, 411.6 us)
Async XLA Ops:
  7.2 86.5 %all-gather.23.cloned.1.call-start = ((), (), s32[]{:S(2)}) async-start(), calls=%async_computation.15 | async-start | bytes 1769472 | tf_op jit(solution)/shard_map/all_gather | solution.py:16
  9.0 129.7 %all-gather.31.cloned.1.call-start = ((), (), s32[]{:S(2)}) async-start(), calls=%async_computation.34 | async-start | bytes 1179648 | tf_op jit(solution)/shard_map/all_gather | solution.py:16
  10.8 142.5 %all-gather.25.cloned.1.call-start = ((), (), s32[]{:S(2)}) async-start(), calls=%async_computation.16 | async-start | bytes 2408448 | tf_op jit(solution)/shard_map/all_gather | solution.py:91
  128.1 46.8 %all-gather.33.cloned.1.call-start = ((), (), s32[]{:S(2)}) async-start(), calls=%async_computation.35 | async-start | bytes 1179648 | tf_op jit(solution)/shard_map/all_gather | solution.py:16
  128.9 95.0 %reduce-scatter.16.cloned.1.call-start = ((), (), s32[]{:S(2)}) async-start(), calls=%async_computation.17 | async-start | bytes 4816896 | tf_op jit(solution)/shard_map/reduce_scatter | solution.py:95
  181.6 74.0 %all-gather.35.cloned.1.call-start = ((), (), s32[]{:S(2)}) async-start(), calls=%async_computation.36 | async-start | bytes 1179648 | tf_op jit(solution)/shard_map/all_gather | solution.py:16
  182.2 98.2 %all-gather.27.cloned.1.call-start = ((), (), s32[]{:S(2)}) async-start(), calls=%async_computation.18 | async-start | bytes 2408448 | tf_op jit(solution)/shard_map/all_gather | solution.py:91
  254.8 47.4 %all-gather.37.cloned.1.call-start = ((), (), s32[]{:S(2)}) async-start(), calls=%async_computation.37 | async-start | bytes 1179648 | tf_op jit(solution)/shard_map/all_gather | solution.py:16
  255.5 95.5 %reduce-scatter.18.cloned.1.call-start = ((), (), s32[]{:S(2)}) async-start(), calls=%async_computation.19 | async-start | bytes 4816896 | tf_op jit(solution)/shard_map/reduce_scatter | solution.py:95
  308.7 75.9 %reduce-scatter.20.cloned.1.call-start = ((), (), s32[]{:S(2)}) async-start(), calls=%async_computation.20 | async-start | bytes 98304 | tf_op jit(solution)/shard_map/reduce_scatter | solution.py:119
  376.3 78.3 %reduce-scatter.22.cloned.1.call-start = ((), (), s32[]{:S(2)}) async-start(), calls=%async_computation.21 | async-start | bytes 4816896 | tf_op jit(solution)/shard_map/reduce_scatter | solution.py:137
  412.3 116.5 %all-gather.29.cloned.1.call-start = ((), (), s32[]{:S(2)}) async-start(), calls=%async_computation.22 | async-start | bytes 2408448 | tf_op jit(solution)/shard_map/all_gather | solution.py:129
  503.2 85.6 %reduce-scatter.24.cloned.1.call-start = ((), (), s32[]{:S(2)}) async-start(), calls=%async_computation.23 | async-start | bytes 4816896 | tf_op jit(solution)/shard_map/reduce_scatter | solution.py:137
  546.5 106.1 %reduce-scatter.38.cloned.1.call-start = ((), (), s32[]{:S(2)}) async-start(), calls=%async_computation.30 | async-start | bytes 2359296 | tf_op jit(solution)/shard_map/reduce_scatter | solution.py:24
  553.1 112.5 %reduce-scatter.36.cloned.1.call-start = ((), (), s32[]{:S(2)}) async-start(), calls=%async_computation.29 | async-start | bytes 2359296 | tf_op jit(solution)/shard_map/reduce_scatter | solution.py:24
  559.1 145.0 %reduce-scatter.42.cloned.1.call-start = ((), (), s32[]{:S(2)}) async-start(), calls=%async_computation.32 | async-start | bytes 2359296 | tf_op jit(solution)/shard_map/reduce_scatter | solution.py:24
  564.9 177.6 %reduce-scatter.40.cloned.1.call-start = ((), (), s32[]{:S(2)}) async-start(), calls=%async_computation.31 | async-start | bytes 2359296 | tf_op jit(solution)/shard_map/reduce_scatter | solution.py:24
  571.3 203.0 %reduce-scatter.30.cloned.1.call-start = ((), (), s32[]{:S(2)}) async-start(), calls=%async_computation.26 | async-start | bytes 147456 | tf_op jit(solution)/shard_map/reduce_scatter | solution.py:24
  576.2 228.8 %reduce-scatter.34.cloned.1.call-start = ((), (), s32[]{:S(2)}) async-start(), calls=%async_computation.28 | async-start | bytes 147456 | tf_op jit(solution)/shard_map/reduce_scatter | solution.py:24
  580.6 255.1 %reduce-scatter.28.cloned.1.call-start = ((), (), s32[]{:S(2)}) async-start(), calls=%async_computation.25 | async-start | bytes 147456 | tf_op jit(solution)/shard_map/reduce_scatter | solution.py:24
  636.0 230.6 %reduce-scatter.32.cloned.1.call-start = ((), (), s32[]{:S(2)}) async-start(), calls=%async_computation.27 | async-start | bytes 147456 | tf_op jit(solution)/shard_map/reduce_scatter | solution.py:24
  637.5 272.8 %reduce-scatter.26.cloned.1.call-start = ((), (), s32[]{:S(2)}) async-start(), calls=%async_computation.24 | async-start | bytes 3538944 | tf_op jit(solution)/shard_map/reduce_scatter | solution.py:24
  648.9 95.4 %copy-start.49 = (f32[256]{0:T(256)S(1)}, f32[256]{0:T(256)}, u32[]{:S(2)}) copy-start(f32[256]{0:T(256)} %get-tuple-element.85) | copy-start | bytes 3076
  649.1 295.2 %reduce-scatter.44.cloned.1.call-start = ((), (), s32[]{:S(2)}) async-start(), calls=%async_computation.33 | async-start | bytes 1179648 | tf_op jit(solution)/shard_map/reduce_scatter | solution.py:24
  (76 other events, 2372.1 us)
Sparse Core Ops, SparseCore 0:
  10.4 24.6 all-gather.22
  37.5 19.6 all-gather.30
  128.2 25.0 all-gather.24
  155.6 19.3 all-gather.32
  181.7 42.1 reduce-scatter.15
  226.2 19.3 all-gather.34
  254.9 25.4 all-gather.26
  282.7 19.3 all-gather.36
  308.8 42.1 reduce-scatter.17
  376.4 8.1 reduce-scatter.19
  412.4 42.1 reduce-scatter.21
  503.3 25.4 all-gather.28
  546.6 42.1 reduce-scatter.23
  591.9 35.2 reduce-scatter.37
  630.3 35.2 reduce-scatter.35
  668.7 35.2 reduce-scatter.41
  707.2 35.2 reduce-scatter.39
  745.9 27.9 reduce-scatter.29
  776.9 28.0 reduce-scatter.33
  807.8 27.9 reduce-scatter.27
  838.7 27.9 reduce-scatter.31
  870.0 40.2 reduce-scatter.25
  914.0 30.2 reduce-scatter.43
where the time goes:
time: 963 us; the launch traced here: 952 us
  waiting for transfers between devices  439 us (46%)
  blocking collectives  253 us (26%)
  matrix products  162 us (17%)
  other arithmetic  55.9 us (6%)
  local copies, waits for them, and re-layouts  21.3 us (2%)
  between operations  19.3 us (2%)
    reduce_scatter x10, waiting for transfers between devices, sum_to_piece(): lax.psum_scatter(grad_full, 'fsdp', scatter_dimension=axis, tiled=True)  245 us
    dot_general x29, matrix products, product(): return jnp.einsum(form, left, right, preferred_element_type=jnp.float32)  162 us
    all_gather x7, blocking collectives, gather_vector(): return lax.all_gather(values, 'fsdp', axis=values.ndim - 1, tiled=True)  61.8 us
    reduce_scatter x2, waiting for transfers between devices, step(): lax.psum_scatter(product('bsd,cd->bsc', d_ch_pre_bf, ch_w1), 'tp', scatte...  50.4 us
    reduce_scatter x2, waiting for transfers between devices, step(): lax.psum_scatter(part_sum, 'tp', scatter_dimension=2, tiled=True)  46.1 us
    all_gather x5, blocking collectives, gather_weight(): lax.all_gather(weight.astype(jnp.bfloat16), 'fsdp', axis=axis, tiled=True)  45 us
    psum x5, blocking collectives, norm_backward(): moments = lax.psum(moments, 'tp') / width  41.9 us
    all_gather x2, waiting for transfers between devices, step(): lax.all_gather(normed2.astype(jnp.bfloat16), 'tp', axis=2, tiled=True)  39.4 us
  transfers between devices with their start and end apart: 23, of which 18 were waited for; matrix products, arithmetic and copies ran while one was open for 16% of the time, Pallas kernels for 0%

commit v1 on v0

v1 whole, which is shorter than its diff:
```python
import functools

import jax
import jax.numpy as jnp
from jax import lax
from jax.experimental import pallas as pl
from jax.experimental.pallas import tpu as pltpu
from jax.sharding import PartitionSpec as P

EPS = 1e-6
CHANNEL_AXES = ('tp', 'fsdp')
LAYER_NAMES = ('ln1_g', 'ln1_b', 'w_tok1', 'b_tok1', 'w_tok2', 'ln2_g', 'ln2_b', 'w_ch1', 'b_ch1', 'w_ch2', 'b_ch2')
MESH = pl.DeviceIdType.MESH
BF16 = jnp.bfloat16
F32 = jnp.float32
ORDERS = ((0, 1, 2), (1, 2, 0), (2, 0, 1))


def product(form, left, right):
    return jnp.einsum(form, left, right, preferred_element_type=jnp.float32)


def my_position():
    tp, fsdp = lax.axis_index('tp'), lax.axis_index('fsdp')
    return (lax.rem(fsdp // 2, 2), fsdp // 4, tp), lax.rem(fsdp, 2)


def shifted(coords, bits):
    return tuple(1 - c if b else c for c, b in zip(coords, bits))


def owner_of(coords, core):
    x, y, z = coords
    return z, y * 4 + x * 2 + core


def device_of(coords, core):
    tp, fsdp = owner_of(coords, core)
    return {'tp': tp, 'fsdp': fsdp}


def unit(dim):
    return tuple(1 if d == dim else 0 for d in range(3))


def plus(a, b):
    return tuple((i + j) % 2 for i, j in zip(a, b))


def entry_barrier(coords, core):
    barrier = pltpu.get_barrier_semaphore()
    for dim in range(3):
        pl.semaphore_signal(barrier, inc=1, device_id=device_of(shifted(coords, unit(dim)), core), device_id_type=MESH)
    pl.semaphore_signal(barrier, inc=1, device_id=device_of(coords, 1 - core), device_id_type=MESH)
    pl.semaphore_wait(barrier, 4)


def stem_block(ref, tp, fsdp, lo, num):
    return ref.at[pl.ds(pl.multiple_of(fsdp * 384 + lo, 16), num), pl.ds(pl.multiple_of(tp * 256, 128), 256)]


def ch1_block(ref, tp, fsdp, lo, num):
    return ref.at[:, pl.ds(pl.multiple_of(fsdp * 64 + lo, 8), num), pl.ds(pl.multiple_of(tp * 1024, 128), 1024)]


def ch2_block(ref, tp, fsdp, lo, num):
    return ref.at[:, pl.ds(pl.multiple_of((tp * 8 + fsdp) * 128 + lo, 8), num), :]


def head_block(ref, tp, fsdp, lo, num):
    return ref.at[pl.ds(pl.multiple_of(fsdp * 64 + lo, 8), num), pl.ds(pl.multiple_of(tp * 512, 128), 512)]


def small_block(ref, tp, fsdp, lo, num):
    return ref.at[tp * 8 + fsdp, pl.ds(lo, num), :]


BLOCKS = (stem_block, small_block, ch1_block, ch2_block, head_block)
GATHER_SPLITS = (((0, 128), (128, 128), (256, 128)), ((0, 24), (24, 24), (48, 16)),
                 ((0, 16), (16, 16), (32, 32)), ((0, 48), (48, 48), (96, 32)), ((0, 32), (32, 16), (48, 16)))
LAYERED = (False, False, True, True, False)


def rows_of(ref, layered, lo, num):
    return ref.at[:, pl.ds(lo, num), :] if layered else ref.at[pl.ds(lo, num), :]


def gather_kernel(*refs):
    own, full = refs[:5], refs[5:10]
    send_sem, recv_sem, local_sem = refs[10:]
    coords, core = my_position()
    entry_barrier(coords, core)
    pending = []

    def move(item, part, bits, src_is_own, target_coords, target_core, sem_index):
        lo, num = GATHER_SPLITS[item][part]
        tp, fsdp = owner_of(shifted(coords, bits), core)
        there = BLOCKS[item](full[item], tp, fsdp, lo, num)
        here = rows_of(own[item], LAYERED[item], lo, num) if src_is_own else there
        copy = pltpu.make_async_remote_copy(
            src_ref=here, dst_ref=there, send_sem=send_sem, recv_sem=recv_sem.at[item, part, sem_index],
            device_id=device_of(target_coords, target_core), device_id_type=MESH)
        copy.start()
        pending.append(copy)

    def arrival(item, part, bits, from_core, sem_index):
        lo, num = GATHER_SPLITS[item][part]
        tp, fsdp = owner_of(shifted(coords, bits), from_core)
        there = BLOCKS[item](full[item], tp, fsdp, lo, num)
        pltpu.make_async_remote_copy(
            src_ref=there, dst_ref=there, send_sem=send_sem, recv_sem=recv_sem.at[item, part, sem_index],
            device_id=device_of(coords, core), device_id_type=MESH).wait_recv()

    def pass_on(item, part, bits, level):
        order = ORDERS[part]
        rank = sum(2 ** i for i in range(3) if bits[order[i]])
        for step in range(level, 3):
            target = shifted(coords, unit(order[step]))
            move(item, part, bits, level == 0, target, core, (0, 1, 3)[step] + rank)
        move(item, part, bits, level == 0, coords, 1 - core, 7 + rank)

    for item in range(5):
        for part in range(3):
            pass_on(item, part, (0, 0, 0), 0)
    locals_ = []
    for item in range(5):
        tp, fsdp = owner_of(coords, core)
        nrows = own[item].shape[-2]
        copy = pltpu.make_async_copy(own[item], BLOCKS[item](full[item], tp, fsdp, 0, nrows), local_sem.at[item])
        copy.start()
        locals_.append(copy)
    for level in range(3):
        for item in range(5):
            for part in range(3):
                order = ORDERS[part]
                for sub in range(2 ** level):
                    bits = [0, 0, 0]
                    for i in range(level):
                        if (sub >> i) % 2:
                            bits[order[i]] = 1
                    arrived = plus(tuple(bits), unit(order[level]))
                    arrival(item, part, arrived, core, (0, 1, 3)[level] + sub)
                    pass_on(item, part, arrived, level + 1)
    for item in range(5):
        for part in range(3):
            order = ORDERS[part]
            for rank in range(8):
                bits = [0, 0, 0]
                for i in range(3):
                    if (rank >> i) % 2:
                        bits[order[i]] = 1
                arrival(item, part, tuple(bits), 1 - core, 7 + rank)
    for copy in locals_:
        copy.wait()
    for copy in pending:
        copy.wait_send()


def gather_all(own):
    any_spec = pl.BlockSpec(memory_space=pl.ANY)
    shapes = [jax.ShapeDtypeStruct((3072, 512), BF16), jax.ShapeDtypeStruct((16, 64, 128), F32),
              jax.ShapeDtypeStruct((2, 512, 2048), BF16), jax.ShapeDtypeStruct((2, 2048, 512), BF16),
              jax.ShapeDtypeStruct((512, 1024), BF16)]
    return pl.pallas_call(
        gather_kernel, out_shape=shapes, in_specs=[any_spec] * 5, out_specs=[any_spec] * 5,
        scratch_shapes=[pltpu.SemaphoreType.DMA, pltpu.SemaphoreType.DMA((5, 3, 15)), pltpu.SemaphoreType.DMA((5,))],
        compiler_params=pltpu.CompilerParams(collective_id=0, has_side_effects=True),
        cost_estimate=pl.CostEstimate(flops=10 ** 9, bytes_accessed=25 * 10 ** 6, transcendentals=0),
        name='gather_weights')(*own)


SUM_SPLITS = (((0, 128), (128, 128), (256, 128)), ((0, 24), (24, 24), (48, 16)),
              ((0, 24), (24, 24), (48, 16)), ((0, 40), (40, 40), (80, 48)), ((0, 24), (24, 24), (48, 16)))
SUM_SHAPES = ((384, 256), (64, 128), (2, 64, 1024), (2, 128, 512), (64, 512))
SUM_ORDER = (4, 3, 2, 0, 1)


BOTH = range(2)


def all_bits():
    return [(x, y, z) for z in BOTH for y in BOTH for x in BOTH]


def sum_kernel(*refs):
    full, out = refs[:5], refs[5:10]
    mine, peer = refs[10:15], refs[15:20]
    inbox = refs[20:65]
    send_sem, peer_sem, load_sem, recv_sem = refs[65:]
    coords, core = my_position()
    entry_barrier(coords, core)
    pending = []
    loads = {}

    def box(item, part, phase):
        return inbox[item * 9 + part * 3 + phase]

    for item in SUM_ORDER:
        for index, bits in enumerate(all_bits()):
            x, y, z = bits
            tp, fsdp = owner_of(shifted(coords, bits), 1 - core)
            nrows = SUM_SHAPES[item][-2]
            copy = pltpu.make_async_remote_copy(
                src_ref=BLOCKS[item](full[item], tp, fsdp, 0, nrows), dst_ref=peer[item].at[z, y, x],
                send_sem=send_sem, recv_sem=peer_sem.at[item, index],
                device_id=device_of(coords, 1 - core), device_id_type=MESH)
            copy.start()
            pending.append(copy)
            tp, fsdp = owner_of(shifted(coords, bits), core)
            load = pltpu.make_async_copy(BLOCKS[item](full[item], tp, fsdp, 0, nrows), mine[item].at[z, y, x],
                                         load_sem.at[item, index])
            load.start()
            loads[item, index] = (copy, load)

    def view(ref, item, part, select):
        lo, num = SUM_SPLITS[item][part]
        z, y, x = select[2], select[1], select[0]
        if LAYERED[item]:
            return ref.at[z, y, x, :, pl.ds(lo, num), :]
        return ref.at[z, y, x, pl.ds(lo, num), :]

    def send_phase(item, part, phase):
        order = ORDERS[part]
        select = [slice(None)] * 3
        for i in range(phase):
            select[order[i]] = 0
        select[order[phase]] = 1
        copy = pltpu.make_async_remote_copy(
            src_ref=view(mine[item], item, part, select), dst_ref=box(item, part, phase),
            send_sem=send_sem, recv_sem=recv_sem.at[item, part, phase],
            device_id=device_of(shifted(coords, unit(order[phase])), core), device_id_type=MESH)
        copy.start()
        pending.append(copy)
        return copy

    copies = {}
    for item in SUM_ORDER:
        for index in range(8):
            copy, load = loads[item, index]
            load.wait()
            copy.wait_recv()

        @pl.loop(0, 8)
        def _(i):
            z, y, x = i // 4, lax.rem(i // 2, 2), lax.rem(i, 2)
            mine[item][z, y, x] = mine[item][z, y, x] + peer[item][z, y, x]
        for part in range(3):
            copies[item, part, 0] = send_phase(item, part, 0)
    for phase in range(3):
        for item in SUM_ORDER:
            for part in range(3):
                copies[item, part, phase].wait_recv()
                order = ORDERS[part]
                rest = [d for d in range(3) if d not in order[:phase + 1]]
                select = [0, 0, 0]
                buf = box(item, part, phase)
                for sub in range(2 ** len(rest)):
                    where = list(select)
                    index = []
                    for j, d in enumerate(sorted(rest, reverse=True)):
                        bit = (sub >> j) % 2
                        where[d] = bit
                        index.append(bit)
                    dst = view(mine[item], item, part, where)
                    src = buf.at[tuple(index)] if index else buf
                    dst[...] = dst[...] + src[...]
                if phase < 2:
                    copies[item, part, phase + 1] = send_phase(item, part, phase + 1)
    for item in range(5):
        out[item][...] = mine[item][0, 0, 0]
    for copy in pending:
        copy.wait_send()


def sum_all(full):
    any_spec = pl.BlockSpec(memory_space=pl.ANY)
    vmem = pl.BlockSpec(memory_space=pltpu.VMEM)
    boxes = []
    for item in range(5):
        for part in range(3):
            num = SUM_SPLITS[item][part][1]
            shape = SUM_SHAPES[item][:-2] + (num, SUM_SHAPES[item][-1])
            for phase in range(3):
                boxes.append(pltpu.VMEM((2,) * (2 - phase) + shape, F32))
    slots = [pltpu.VMEM((2, 2, 2) + s, F32) for s in SUM_SHAPES]
    return pl.pallas_call(
        sum_kernel, out_shape=[jax.ShapeDtypeStruct(s, F32) for s in SUM_SHAPES],
        in_specs=[any_spec] * 5, out_specs=[vmem] * 5,
        scratch_shapes=slots + slots + boxes + [
            pltpu.SemaphoreType.DMA, pltpu.SemaphoreType.DMA((5, 8)), pltpu.SemaphoreType.DMA((5, 8)),
            pltpu.SemaphoreType.DMA((5, 3, 3))],
        compiler_params=pltpu.CompilerParams(collective_id=1, has_side_effects=True, vmem_limit_bytes=63 * 2 ** 20),
        cost_estimate=pl.CostEstimate(flops=10 ** 9, bytes_accessed=50 * 10 ** 6, transcendentals=0),
        name='sum_gradients')(*full)


VECTORS = (('b_stem', 1), ('lnf_g', 1), ('lnf_b', 1), ('ln1_g', 2), ('ln1_b', 2), ('ln2_g', 2), ('ln2_b', 2), ('b_ch2', 2))


def pack_own(weights):
    pieces = [weights[name].reshape(-1) for name, _ in VECTORS]
    pieces += [weights[name].reshape(-1) for name in ('b_ch1', 'b_tok1', 'w_tok1', 'w_tok2', 'b_head')]
    flat = jnp.concatenate(pieces)
    return jnp.pad(flat, (0, 8192 - flat.shape[0])).reshape(64, 128)


def unpack_full(packed):
    rows = packed.reshape(16, 8192)
    found = {}
    at = 0
    for name, num in VECTORS:
        found[name] = rows[:, at:at + num * 32].reshape(16, num, 32).swapaxes(0, 1).reshape(num, 512)
        at += num * 32
    found['b_ch1'] = rows[:, at:at + 256].reshape(16, 2, 128).swapaxes(0, 1).reshape(2, 2048)
    at += 256
    half = rows[:8]
    found['b_tok1'] = half[:, at:at + 64].reshape(8, 2, 32).swapaxes(0, 1).reshape(2, 256)
    at += 64
    found['w_tok1'] = half[:, at:at + 3136].reshape(8, 2, 49, 32).transpose(1, 2, 0, 3).reshape(2, 49, 256)
    at += 3136
    found['w_tok2'] = half[:, at:at + 3136].reshape(8, 2, 32, 49).swapaxes(0, 1).reshape(2, 256, 49)
    at += 3136
    found['b_head'] = jnp.pad(rows[::8, at:at + 500], ((0, 0), (0, 12))).reshape(1024)
    return found


def pack_grads(grads, loss):
    pieces = [grads[name].reshape(num, 16, 32).swapaxes(0, 1).reshape(16, num * 32) for name, num in VECTORS]
    pieces.append(grads['b_ch1'].reshape(2, 16, 128).swapaxes(0, 1).reshape(16, 256))

    def twice(values):
        return jnp.concatenate([values, values], axis=0)
    pieces.append(twice(grads['b_tok1'].reshape(2, 8, 32).swapaxes(0, 1).reshape(8, 64)))
    pieces.append(twice(grads['w_tok1'].reshape(2, 49, 8, 32).transpose(2, 0, 1, 3).reshape(8, 3136)))
    pieces.append(twice(grads['w_tok2'].reshape(2, 8, 32, 49).swapaxes(0, 1).reshape(8, 3136)))
    pieces.append(jnp.repeat(grads['b_head'].reshape(2, 512)[:, :500], 8, axis=0))
    pieces.append(jnp.broadcast_to(loss.reshape(1, 1), (16, 1)))
    flat = jnp.concatenate(pieces, axis=1)
    return jnp.pad(flat, ((0, 0), (0, 8192 - flat.shape[1]))).reshape(16, 64, 128)


def unpack_own(packed):
    flat = packed.reshape(-1)
    found = {}
    at = 0
    for name, num in VECTORS:
        found[name] = flat[at:at + num * 32].reshape((num, 32) if num == 2 else (32,))
        at += num * 32
    for name, shape in (('b_ch1', (2, 128)), ('b_tok1', (2, 32)), ('w_tok1', (2, 49, 32)), ('w_tok2', (2, 32, 49)),
                        ('b_head', (500,)), ('loss', ())):
        size = 1
        for s in shape:
            size *= s
        found[name] = flat[at:at + size].reshape(shape)
        at += size
    return found


def norm_forward(values, gain, shift):
    mean_val = jnp.mean(values, axis=-1, keepdims=True)
    centered = values - mean_val
    inv_std = lax.rsqrt(jnp.mean(centered * centered, axis=-1, keepdims=True) + EPS)
    standard = centered * inv_std
    return standard * gain + shift, standard, inv_std


def norm_backward(grad_out, gain, standard, inv_std):
    grad_std = grad_out * gain
    first = jnp.mean(grad_std, axis=-1, keepdims=True)
    second = jnp.mean(grad_std * standard, axis=-1, keepdims=True)
    return inv_std * (grad_std - first - standard * second)


def gelu_grad(pre_act, grad_out):
    return jax.vjp(jax.nn.gelu, pre_act)[1](grad_out)[0]


def lead_sum(values):
    return jnp.sum(values.reshape(-1, values.shape[-1]), axis=0)


def weight_specs():
    vec_spec = P(CHANNEL_AXES)
    layer_vec = P(None, CHANNEL_AXES)
    return (P('fsdp', 'tp'), vec_spec, layer_vec, layer_vec, P(None, None, 'fsdp'), P(None, 'fsdp'),
            P(None, 'fsdp', None), layer_vec, layer_vec, P(None, 'fsdp', 'tp'), layer_vec,
            P(None, CHANNEL_AXES, None), layer_vec, vec_spec, vec_spec, P('fsdp', 'tp'), P('tp'))


def solution(mesh):
    total_images = 256

    def step(patches, labels, w_stem, b_stem, ln1_g, ln1_b, w_tok1, b_tok1, w_tok2,
             ln2_g, ln2_b, w_ch1, b_ch1, w_ch2, b_ch2, lnf_g, lnf_b, w_head, b_head):
        half = patches.shape[0] // 2
        tp = lax.axis_index('tp')
        patches = lax.dynamic_slice_in_dim(patches, tp * half, half, 0)
        labels = lax.dynamic_slice_in_dim(labels, tp * half, half, 0)
        small_own = pack_own(dict(b_stem=b_stem, lnf_g=lnf_g, lnf_b=lnf_b, ln1_g=ln1_g, ln1_b=ln1_b, ln2_g=ln2_g,
                                  ln2_b=ln2_b, b_ch2=b_ch2, b_ch1=b_ch1, b_tok1=b_tok1, w_tok1=w_tok1, w_tok2=w_tok2,
                                  b_head=b_head))
        head_own = jnp.pad(w_head.astype(BF16), ((0, 0), (0, 12)))
        stem_w, small, ch1_w, ch2_w, head_w = gather_all(
            [w_stem.astype(BF16), small_own, w_ch1.astype(BF16), w_ch2.astype(BF16), head_own])
        small = unpack_full(small)
        tok1_w, tok2_w = small['w_tok1'].astype(BF16), small['w_tok2'].astype(BF16)

        tokens = patches.shape[1]
        resid = product('bsp,pc->bsc', patches, stem_w) + small['b_stem'][0]
        saved = []
        for layer in range(2):
            normed, norm1_std, norm1_inv = norm_forward(resid, small['ln1_g'][layer], small['ln1_b'][layer])
            normed = normed.astype(BF16)
            tok_pre = product('bsc,sj->bjc', normed, tok1_w[layer]) + small['b_tok1'][layer][:, None]
            tok_act = jax.nn.gelu(tok_pre).astype(BF16)
            resid = resid + product('bjc,js->bsc', tok_act, tok2_w[layer])
            normed2, norm2_std, norm2_inv = norm_forward(resid, small['ln2_g'][layer], small['ln2_b'][layer])
            full_in = normed2.astype(BF16)
            ch_pre = product('bsc,cd->bsd', full_in, ch1_w[layer]) + small['b_ch1'][layer]
            ch_act = jax.nn.gelu(ch_pre).astype(BF16)
            resid = resid + product('bsd,dc->bsc', ch_act, ch2_w[layer]) + small['b_ch2'][layer]
            saved.append(dict(normed=normed, norm1_std=norm1_std, norm1_inv=norm1_inv, tok_pre=tok_pre,
                              tok_act=tok_act, norm2_std=norm2_std, norm2_inv=norm2_inv,
                              full_in=full_in, ch_pre=ch_pre, ch_act=ch_act))

        pooled = jnp.mean(resid, axis=1)
        head_in, head_std, head_inv = norm_forward(pooled, small['lnf_g'][0], small['lnf_b'][0])
        head_full = head_in.astype(BF16)
        logits = product('bc,ck->bk', head_full, head_w) + small['b_head']
        column = lax.broadcasted_iota(jnp.int32, logits.shape, 1)
        real = lax.rem(column, 512) < 500
        class_ids = (column // 512) * 500 + lax.rem(column, 512)
        is_label = jnp.logical_and(class_ids == labels[:, None], real)
        row_max = jnp.max(jnp.where(real, logits, -jnp.inf), axis=1, keepdims=True)
        exps = jnp.where(real, jnp.exp(jnp.where(real, logits, row_max) - row_max), 0.0)
        sums = jnp.sum(exps, axis=1, keepdims=True)
        picked = jnp.sum(jnp.where(is_label, logits, 0.0), axis=1)
        loss = jnp.sum(row_max[:, 0] + jnp.log(sums[:, 0]) - picked) / total_images

        grads = {}
        d_logits = (exps / sums - is_label.astype(F32)) / total_images
        d_logits_bf = d_logits.astype(BF16)
        g_head = product('bc,bk->ck', head_full, d_logits_bf)
        grads['b_head'] = jnp.sum(d_logits, axis=0)
        d_head_in = product('bk,ck->bc', d_logits_bf, head_w)
        grads['lnf_g'] = jnp.sum(d_head_in * head_std, axis=0)
        grads['lnf_b'] = jnp.sum(d_head_in, axis=0)
        d_pooled = norm_backward(d_head_in, small['lnf_g'][0], head_std, head_inv)
        d_resid = jnp.broadcast_to((d_pooled / tokens)[:, None, :], resid.shape)

        lists = {name: [] for name in LAYER_NAMES}
        for layer in (1, 0):
            keep = saved[layer]
            lists['b_ch2'].append(lead_sum(d_resid))
            d_out = d_resid.astype(BF16)
            lists['w_ch2'].append(product('bsd,bsc->dc', keep['ch_act'], d_out))
            d_ch_pre = gelu_grad(keep['ch_pre'], product('bsc,dc->bsd', d_out, ch2_w[layer]))
            lists['b_ch1'].append(lead_sum(d_ch_pre))
            d_ch_pre_bf = d_ch_pre.astype(BF16)
            lists['w_ch1'].append(product('bsc,bsd->cd', keep['full_in'], d_ch_pre_bf))
            d_norm2 = product('bsd,cd->bsc', d_ch_pre_bf, ch1_w[layer])
            lists['ln2_g'].append(lead_sum(d_norm2 * keep['norm2_std']))
            lists['ln2_b'].append(lead_sum(d_norm2))
            d_mid = d_resid + norm_backward(d_norm2, small['ln2_g'][layer], keep['norm2_std'], keep['norm2_inv'])
            d_mid_bf = d_mid.astype(BF16)
            lists['w_tok2'].append(product('bjc,bsc->js', keep['tok_act'], d_mid_bf))
            d_tok_pre = gelu_grad(keep['tok_pre'], product('bsc,js->bjc', d_mid_bf, tok2_w[layer]))
            lists['b_tok1'].append(jnp.sum(d_tok_pre, axis=(0, 2)))
            d_tok_pre_bf = d_tok_pre.astype(BF16)
            lists['w_tok1'].append(product('bsc,bjc->sj', keep['normed'], d_tok_pre_bf))
            d_norm1 = product('bjc,sj->bsc', d_tok_pre_bf, tok1_w[layer])
            lists['ln1_g'].append(lead_sum(d_norm1 * keep['norm1_std']))
            lists['ln1_b'].append(lead_sum(d_norm1))
            d_resid = d_mid + norm_backward(d_norm1, small['ln1_g'][layer], keep['norm1_std'], keep['norm1_inv'])

        grads['b_stem'] = lead_sum(d_resid)
        g_stem = product('bsp,bsc->pc', patches, d_resid.astype(BF16))
        for name in LAYER_NAMES:
            grads[name] = jnp.stack(lists[name][::-1])
        o_stem, o_small, o_ch1, o_ch2, o_head = sum_all(
            [g_stem, pack_grads(grads, loss), grads['w_ch1'], grads['w_ch2'], g_head])
        found = unpack_own(o_small)
        found['w_ch1'], found['w_ch2'] = o_ch1, o_ch2
        return tuple([found['loss'], o_stem, found['b_stem']] + [found[name] for name in LAYER_NAMES]
                     + [found['lnf_g'], found['lnf_b'], o_head[:, :500], found['b_head']])

    specs = weight_specs()
    return jax.shard_map(step, mesh=mesh, in_specs=(P('fsdp', None, None), P('fsdp')) + specs,
                         out_specs=(P(),) + specs, check_vma=False)
```

time: 963 us -> 343 us (0.36)
  waiting for transfers between devices: 439 us -> 0 us
  blocking collectives: 253 us -> 0 us
  Pallas kernels: 0 us -> 142 us
  matrix products: 162 us -> 121 us
  other arithmetic: 55.9 us -> 21.9 us
  local copies, waits for them, and re-layouts: 21.3 us -> 49.9 us
  between operations: 19.3 us -> 3.49 us
    reduce_scatter x15 -> x0, waiting for transfers between devices: 349 us -> none  [the longest x10 245 us: sum_to_piece(): lax.psum_scatter(grad_full, 'fsdp', scatter_dimension=axis, tiled=True)]
    pallas_call x0 -> x2, Pallas kernels: none -> 142 us  [the longest x1 92 us: sum_all(): pl.pallas_call(sum_kernel, out_shape=[jax.ShapeDtypeStruct(s, F32) for s...]
    psum x13 -> x0, blocking collectives: 119 us -> none  [the longest x5 41.9 us: norm_backward(): moments = lax.psum(moments, 'tp') / width]
    all_gather x14 -> x0, blocking collectives: 116 us -> none  [the longest x7 61.8 us: gather_vector(): return lax.all_gather(values, 'fsdp', axis=values.ndim - 1, tiled=True)]
    all_gather x8 -> x0, waiting for transfers between devices: 88.4 us -> none  [the longest x2 39.4 us: step(): lax.all_gather(normed2.astype(jnp.bfloat16), 'tp', axis=2, tiled=True)]
    dot_general x29, matrix products: 162 us -> 121 us  [product(): return jnp.einsum(form, left, right, preferred_element_type=jnp.float32)]
    unnamed x1 -> x0, blocking collectives: 13.7 us -> none
    convert_element_type x11 -> x5, other arithmetic: 14.3 us -> 2.26 us  [the longest x1 0.74 us: step(): w_ch1.astype(BF16)]
  transfers between devices with their start and end apart: 23 -> 0, of which waited for: 18 -> 0; matrix products, arithmetic and copies ran while one was open for 16% -> 0% of each run, Pallas kernels for 0% -> 0%
where the time goes in v1:
time: 343 us; the launch traced here: 339 us
  Pallas kernels  142 us (41%)
  matrix products  121 us (35%)
  local copies, waits for them, and re-layouts  49.9 us (15%)
  other arithmetic  21.9 us (6%)
  between operations  3.49 us (1%)
    dot_general x29, matrix products, product(): return jnp.einsum(form, left, right, preferred_element_type=jnp.float32)  121 us
    pallas_call x1, Pallas kernels, sum_all(): pl.pallas_call(sum_kernel, out_shape=[jax.ShapeDtypeStruct(s, F32) for s...  92 us
    pallas_call x1, Pallas kernels, gather_all(): pl.pallas_call(gather_kernel, out_shape=shapes, in_specs=[any_spec] * 5,...  50.1 us
    unnamed x227, local copies, waits for them, and re-layouts  26.8 us
    another operation x3, other arithmetic, step(): grads[name] = jnp.stack(lists[name][::-1])  8.38 us

profile of v1, /device:TPU:0, one launch (start us, length us, event | category | flops | bytes accessed | tf_op | source)
XLA Modules:
  0.0 338.7 jit_solution(12934236123950701441)
XLA Ops:
  0.8 5.3 %constant_dynamic-slice_fusion = bf16[16,49,3072]{2,0,1:T(8,128)(2,1)} fusion(bf16[32,49,3072]{2,0,1:T(8,128)(2,1)} %param.19, s32[]{:T(128)S(6)} %select_n.23), kind=kLoop, calls=%fused_computation.225 | loop fusion | bytes 9633796 | tf_op jit(solution)/shard_map/dynamic_slice | solution.py:397
  10.5 50.1 %gather_weights.1 = (bf16[3072,512]{1,0:T(8,128)(2,1)}, f32[16,64,128]{2,1,0:T(8,128)}, bf16[2,512,2048]{2,1,0:T(8,128)(2,1)}, bf16[2,2048,512]{2,1,0:T(8,128)(2,1)}, bf16[512,1024]{1,0:T(8,128)(2,1)}) custom-call(bf16[384,256]{1,0:T(8,128)(2,1)} %convert_element_type.97.refs_0_, f32[64,128]{1,0:T(8,128)} %pad_bitcast_fusion.1.refs_1_, ...), custom_call_target="tpu_custom_call" | custom-call | flops 1000000000 | bytes 25000000 | tf_op jit(solution)/shard_map/gather_weights/pallas_call | solution.py:164
  66.1 7.5 %add_reduce_fusion.1 = (f32[16,49]{1,0:T(8,128)S(1)}, f32[16,49,512]{2,1,0:T(8,128)S(1)}) fusion(f32[512]{0:T(512)S(1)} %add.257, bf16[3072,512]{1,0:T(8,128)(2,1)} %get-tuple-element.28, bf16[16,49,3072]{2,0,1:T(8,128)(2,1)} %constant_dynamic-slice_fusion), kind=kOutput, calls=%fused_computation.130 | convolution fusion | flops 2467052800 | bytes 9573440 | tf_op jit(solution)/shard_map/bsp,pc->bsc/dot_general | solution.py:20
  74.1 5.6 %fusion.19 = (bf16[16,256,512]{2,1,0:T(8,128)(2,1)S(1)}, f32[256,16,512]{2,0,1:T(8,128)}) fusion(f32[256]{0:T(256)S(1)} %add.264, bf16[49,256,1]{0,1,2:T(8,128)(2,1)S(1)} %bitcast.270, f32[512]{0:T(512)S(1)} %add.261, f32[512]{0:T(512)S(1)} %mul.418, f32[16,49]{1,0:T(8,128)S(1)} %add_rsqrt_fusion.3, f32[16,49]{1,0:T(8,128)S(1)} %broadcast_multiply_fusion.11, ...), kind=kOutput, calls=%fused_computation.35 | convolution fusion | flops 228900864 | bytes 14227072 | tf_op jit(solution)/shard_map/bsc,sj->bjc/dot_general | solution.py:20
  82.2 6.8 %fusion.52 = f32[16,49,2048]{2,1,0:T(8,128)} fusion(bf16[2,512,2048]{2,1,0:T(8,128)(2,1)} %get-tuple-element.30, f32[16,49,512]{2,1,0:T(8,128)S(1)} %get-tuple-element.146, f32[512]{0:T(512)S(1)} %add.272, f32[512]{0:T(512)S(1)} %mul.428, f32[16,49]{1,0:T(8,128)S(1)} %add_rsqrt_fusion.2, f32[16,49]{1,0:T(8,128)S(1)} %broadcast_multiply_fusion.10), kind=kOutput, calls=%fused_computation.72 | convolution fusion | flops 1646174208 | bytes 10135680 | tf_op jit(solution)/shard_map/bsc,cd->bsd/dot_general | solution.py:20
  89.2 7.4 %fusion.119 = (f32[16,49]{1,0:T(8,128)S(1)}, f32[16,49,512]{2,1,0:T(8,128)S(1)}) fusion(f32[512]{0:T(512)S(1)} %add.281, f32[16,49,512]{2,1,0:T(8,128)} %copy-done.7, bf16[2,2048,512]{2,1,0:T(8,128)(2,1)} %get-tuple-element.31, f32[16,49,2048]{2,1,0:T(8,128)} %fusion.52, f32[2048]{0:T(1024)S(1)} %bitcast.294), kind=kOutput, calls=%fused_computation.242 | convolution fusion | flops 1661426944 | bytes 12891200 | tf_op jit(solution)/shard_map/bsd,dc->bsc/dot_general | solution.py:20
  97.3 6.0 %fusion.18 = (bf16[16,256,512]{2,1,0:T(8,128)(2,1)S(1)}, f32[256,16,512]{2,0,1:T(8,128)}) fusion(f32[256]{0:T(256)S(1)} %add.288, bf16[49,256,1]{0,1,2:T(8,128)(2,1)S(1)} %bitcast.274, f32[16,49,512]{2,1,0:T(8,128)S(1)} %get-tuple-element.148, f32[512]{0:T(512)S(1)} %add.285, f32[512]{0:T(512)S(1)} %mul.438, f32[16,49]{1,0:T(8,128)S(1)} %add_rsqrt_fusion.1, ...), kind=kOutput, calls=%fused_computation.33 | convolution fusion | flops 228499456 | bytes 14225024 | tf_op jit(solution)/shard_map/bsc,sj->bjc/dot_general | solution.py:20
  109.5 4.5 %fusion.45 = f32[16,49,2048]{2,1,0:T(8,128)S(1)} fusion(bf16[2,512,2048]{2,1,0:T(8,128)(2,1)} %get-tuple-element.30, f32[16,49,512]{2,1,0:T(8,128)} %get-tuple-element.152, f32[512]{0:T(512)S(1)} %add.296, f32[512]{0:T(512)S(1)} %mul.448, f32[16,49]{1,0:T(8,128)S(1)} %add_rsqrt_fusion, f32[16,49]{1,0:T(8,128)S(1)} %broadcast_multiply_fusion.8), kind=kOutput, calls=%fused_computation.65 | convolution fusion | flops 1646174208 | bytes 10365056 | tf_op jit(solution)/shard_map/bsc,cd->bsd/dot_general | solution.py:20
  114.1 3.1 add_reduce_fusion
  120.1 9.3 %fusion.121 = (f32[2048]{0:T(1024)S(1)}, bf16[16,49,2048]{2,1,0:T(8,128)(2,1)S(1)}) fusion(f32[16,49,2048]{2,1,0:T(8,128)} %copy-done.92, f32[2048]{0:T(1024)S(1)} %bitcast.298, bf16[2,2048,512]{2,1,0:T(8,128)(2,1)} %get-tuple-element.31, bf16[16,512]{1,0:T(8,128)(2,1)S(1)} %get-tuple-element.110), kind=kOutput, calls=%fused_computation.244 | convolution fusion | flops 1679489024 | bytes 12681216 | tf_op jit(solution)/shard_map/bsc,dc->bsd/dot_general | solution.py:20
  134.9 7.3 %fusion.123 = (f32[256]{0:T(256)S(1)}, bf16[16,256,512]{2,1,0:T(8,128)(2,1)S(1)}) fusion(f32[256,16,512]{2,0,1:T(8,128)S(1)} %bitcast.310, f32[256]{0:T(256)S(1)} %add.288, bf16[256,49,1]{1,0,2:T(8,128)(2,1)S(1)} %bitcast.273, f32[16,49,512]{2,1,0:T(8,128)S(1)} %get-tuple-element.138), kind=kOutput, calls=%fused_computation.246 | convolution fusion | flops 252059392 | bytes 14215680 | tf_op jit(solution)/shard_map/bsc,js->bjc/dot_general | solution.py:20
  149.4 7.2 %fusion.122 = (f32[2048]{0:T(1024)S(1)}, bf16[16,49,2048]{2,1,0:T(8,128)(2,1)S(1)}) fusion(f32[16,49,2048]{2,1,0:T(8,128)S(1)} %bitcast.304, f32[2048]{0:T(1024)S(1)} %bitcast.295, bf16[2,2048,512]{2,1,0:T(8,128)(2,1)S(1)} %copy-done.95, f32[16,49,512]{2,1,0:T(8,128)S(1)} %get-tuple-element.107), kind=kOutput, calls=%fused_computation.245 | convolution fusion | flops 1679890432 | bytes 14499840 | tf_op jit(solution)/shard_map/bsc,dc->bsd/dot_general | solution.py:20
  156.7 2.6 multiply_reduce_fusion.1
  162.1 7.3 %fusion.124 = (f32[256]{0:T(256)S(1)}, bf16[16,256,512]{2,1,0:T(8,128)(2,1)S(1)}) fusion(f32[256,16,512]{2,0,1:T(8,128)S(1)} %bitcast.308, f32[256]{0:T(256)S(1)} %copy-done.78, bf16[256,49,1]{1,0,2:T(8,128)(2,1)S(1)} %bitcast.269, f32[16,49,512]{2,1,0:T(8,128)S(1)} %multiply_add_fusion.1), kind=kOutput, calls=%fused_computation.247 | convolution fusion | flops 252059392 | bytes 14215680 | tf_op jit(solution)/shard_map/bsc,js->bjc/dot_general | solution.py:20
  173.9 8.1 %fusion.36.refs_0_ = f32[3072,512]{1,0:T(8,128)} fusion(bf16[16,49,3072]{2,0,1:T(8,128)(2,1)S(1)} %bitcast.254, bf16[16,49,512]{2,1,0:T(8,128)(2,1)S(1)} %get-tuple-element.109), kind=kOutput, calls=%fused_computation.54 | convolution fusion | flops 2466250752 | bytes 11911168 | tf_op jit(solution)/shard_map/bsp,bsc->pc/dot_general | solution.py:20
  187.3 3.7 %fusion.58 = f32[49,256,1]{0,1,2:T(8,128)S(1)} fusion(bf16[16,256,512]{2,1,0:T(8,128)(2,1)} %copy-done.5, f32[16,49,512]{2,1,0:T(8,128)S(1)} %get-tuple-element.148, f32[512]{0:T(512)S(1)} %add.285, f32[512]{0:T(512)S(1)} %mul.438, f32[16,49]{1,0:T(8,128)S(1)} %add_rsqrt_fusion.1, f32[16,49]{1,0:T(8,128)S(1)} %broadcast_multiply_fusion.9), kind=kOutput, calls=%fused_computation.78 | convolution fusion | flops 207527936 | bytes 5860480 | tf_op jit(solution)/shard_map/bsc,bjc->sj/dot_general | solution.py:20
  193.2 3.6 %fusion.88 = f32[256,49,1]{1,0,2:T(8,128)S(1)} fusion(bf16[16,256,512]{2,1,0:T(8,128)(2,1)} %copy-done.6, f32[16,49,512]{2,1,0:T(8,128)S(1)} %copy-done.15), kind=kOutput, calls=%fused_computation.141 | convolution fusion | flops 205922304 | bytes 5850112 | tf_op jit(solution)/shard_map/bjc,bsc->js/dot_general | solution.py:20
  201.5 4.8 %convolution_bitcast_fusion.2 = f32[1,512,2048]{2,1,0:T(8,128)S(1)} fusion(bf16[16,49,2048]{2,1,0:T(8,128)(2,1)} %copy-done.89, f32[16,49,512]{2,1,0:T(8,128)S(1)} %copy-done.12, f32[512]{0:T(512)S(1)} %copy-done.75, f32[512]{0:T(512)S(1)} %copy-done.58, f32[16,49]{1,0:T(8,128)S(1)} %add_rsqrt_fusion, f32[16,49]{1,0:T(8,128)S(1)} %broadcast_multiply_fusion.8), kind=kOutput, calls=%fused_computation.57 | convolution fusion | flops 1646174208 | bytes 9021568 | tf_op jit(solution)/shard_map/bsc,bsd->cd/dot_general | solution.py:20
  206.3 2.6 convolution_bitcast_fusion.3
  209.0 4.2 %pad_maximum_fusion.refs_2_ = f32[2,512,2048]{2,1,0:T(8,128)} fusion(f32[1,512,2048]{2,1,0:T(8,128)S(1)} %convolution_bitcast_fusion.2, f32[1,512,2048]{2,1,0:T(8,128)S(1)} %convolution_bitcast_fusion.3), kind=kLoop, calls=%fused_computation.20 | loop fusion | flops 2097152 | bytes 16777216 | tf_op jit(solution)/shard_map/stack | solution.py:479
  213.2 6.5 %convolution_bitcast_fusion = f32[1,2048,512]{2,1,0:T(8,128)S(1)} fusion(bf16[16,512]{1,0:T(8,128)(2,1)S(1)} %get-tuple-element.110, f32[16,49,2048]{2,1,0:T(8,128)} %copy-done.92, f32[2048]{0:T(1024)S(1)} %bitcast.299), kind=kOutput, calls=%fused_computation.55 | convolution fusion | flops 1660223488 | bytes 10641408 | tf_op jit(solution)/shard_map/bsd,bsc->dc/dot_general | solution.py:20
  219.7 4.0 %convolution_bitcast_fusion.1 = f32[1,2048,512]{2,1,0:T(8,128)S(1)} fusion(f32[16,49,512]{2,1,0:T(8,128)S(1)} %copy-done.20, f32[16,49,2048]{2,1,0:T(8,128)S(1)} %bitcast.306, f32[2048]{0:T(1024)S(1)} %bitcast.296), kind=kOutput, calls=%fused_computation.56 | convolution fusion | flops 1660624896 | bytes 12230656 | tf_op jit(solution)/shard_map/bsd,bsc->dc/dot_general | solution.py:20
  223.8 4.2 %pad_maximum_fusion.1.refs_3_ = f32[2,2048,512]{2,1,0:T(8,128)} fusion(f32[1,2048,512]{2,1,0:T(8,128)S(1)} %convolution_bitcast_fusion, f32[1,2048,512]{2,1,0:T(8,128)S(1)} %convolution_bitcast_fusion.1), kind=kLoop, calls=%fused_computation.21 | loop fusion | flops 2097152 | bytes 16777216 | tf_op jit(solution)/shard_map/stack | solution.py:479
  229.9 92.0 %sum_gradients.1 = (f32[384,256]{1,0:T(8,128)}, f32[64,128]{1,0:T(8,128)}, f32[2,64,1024]{2,1,0:T(8,128)}, f32[2,128,512]{2,1,0:T(8,128)}, f32[64,512]{1,0:T(8,128)}) custom-call(f32[3072,512]{1,0:T(8,128)} %fusion.36.refs_0_, f32[16,64,128]{2,1,0:T(8,128)} %bitcast.255, f32[2,512,2048]{2,1,0:T(8,128)} %pad_maximum_fusion.refs_2_, ...), custom_call_target="tpu_custom_call" | custom-call | flops 1000000000 | bytes 50000000 | tf_op jit(solution)/shard_map/sum_gradients/pallas_call | solution.py:286
  (386 shorter events, 71.6 us)
Async XLA Ops:
  0.8 9.1 %copy-start.34 = (f32[64,500]{1,0:T(8,128)S(1)}, f32[64,500]{1,0:T(8,128)}, u32[]{:S(2)}) copy-start(f32[64,500]{1,0:T(8,128)} %param.36) | copy-start | bytes 384004
  62.0 27.0 %copy-start.26 = (f32[2,8,64,128]{3,1,2,0:T(8,128)}, f32[2,8,64,128]{3,1,2,0:T(8,128)S(1)}, u32[]{:S(2)}) copy-start(f32[2,8,64,128]{3,1,2,0:T(8,128)S(1)} %copy.123) | copy-start | bytes 1572868
  64.0 39.3 %copy-start.32 = (bf16[1,8,32,49]{3,2,0,1:T(8,128)(2,1)}, bf16[1,8,32,49]{3,2,0,1:T(8,128)(2,1)S(1)}, u32[]{:S(2)}) copy-start(bf16[1,8,32,49]{3,2,0,1:T(8,128)(2,1)S(1)} %get-tuple-element.128) | copy-start | bytes 75268
  64.4 9.7 %copy-start.77 = (f32[256]{0:T(256)}, f32[256]{0:T(256)S(1)}, u32[]{:S(2)}) copy-start(f32[256]{0:T(256)S(1)} %add.264) | copy-start | bytes 3076
  64.8 9.3 %copy-start.30 = (bf16[1,49,8,32]{1,3,2,0:T(8,128)(2,1)}, bf16[1,49,8,32]{1,3,2,0:T(8,128)(2,1)S(1)}, u32[]{:S(2)}) copy-start(bf16[1,49,8,32]{1,3,2,0:T(8,128)(2,1)S(1)} %copy.63) | copy-start | bytes 75268
  65.1 9.0 %copy-start.72 = (f32[512]{0:T(512)}, f32[512]{0:T(512)S(1)}, u32[]{:S(2)}) copy-start(f32[512]{0:T(512)S(1)} %add.261) | copy-start | bytes 6148
  89.2 30.9 %copy-start.61 = (f32[1,16,128]{2,0,1:T(1,128)}, f32[1,16,128]{2,0,1:T(1,128)S(1)}, u32[]{:S(2)}) copy-start(f32[1,16,128]{2,0,1:T(1,128)S(1)} %get-tuple-element.139) | copy-start | bytes 24580
  89.2 56.1 %copy-start.59 = (f32[1,16,128]{2,0,1:T(1,128)}, f32[1,16,128]{2,0,1:T(1,128)S(1)}, u32[]{:S(2)}) copy-start(f32[1,16,128]{2,0,1:T(1,128)S(1)} %get-tuple-element.140) | copy-start | bytes 24580
  107.6 24.5 %copy-start.57 = (f32[512]{0:T(512)}, f32[512]{0:T(512)S(1)}, u32[]{:S(2)}) copy-start(f32[512]{0:T(512)S(1)} %mul.448) | copy-start | bytes 6148
  117.2 12.1 %copy-start.24 = (f32[16,512]{1,0:T(8,128)}, f32[16,512]{1,0:T(8,128)S(1)}, u32[]{:S(2)}) copy-start(f32[16,512]{1,0:T(8,128)S(1)} %add_reduce_fusion) | copy-start | bytes 98308
  117.4 12.0 %copy-start.53 = (f32[16]{0:T(128)}, f32[16]{0:T(128)S(1)}, u32[]{:S(2)}) copy-start(f32[16]{0:T(128)S(1)} %broadcast_multiply_fusion.14) | copy-start | bytes 196
  117.6 11.8 %copy-start.65 = (f32[16]{0:T(128)}, f32[16]{0:T(128)S(1)}, u32[]{:S(2)}) copy-start(f32[16]{0:T(128)S(1)} %add_rsqrt_fusion.4) | copy-start | bytes 196
  117.7 11.7 %copy-start.35 = (f32[512]{0:T(512)}, f32[512]{0:T(512)S(1)}, u32[]{:S(2)}) copy-start(f32[512]{0:T(512)S(1)} %mul.458) | copy-start | bytes 6148
  117.8 80.9 %copy-start.43 = (pred[1024]{0:T(1024)(128)(4,1)}, pred[1024]{0:T(1024)(128)(4,1)S(1)}, u32[]{:S(2)}) copy-start(pred[1024]{0:T(1024)(128)(4,1)S(1)} %get-tuple-element.175) | copy-start | bytes 3076
  117.8 80.9 %copy-start.51 = (pred[1024]{0:T(1024)(128)(4,1)}, pred[1024]{0:T(1024)(128)(4,1)S(1)}, u32[]{:S(2)}) copy-start(pred[1024]{0:T(1024)(128)(4,1)S(1)} %get-tuple-element.174) | copy-start | bytes 3076
  118.8 10.7 %copy-start.45 = (f32[512]{0:T(512)}, f32[512]{0:T(512)S(1)}, u32[]{:S(2)}) copy-start(f32[512]{0:T(512)S(1)} %add.309) | copy-start | bytes 6148
  119.2 79.8 %copy-start.49 = (f32[16]{0:T(128)}, f32[16]{0:T(128)S(1)}, u32[]{:S(2)}) copy-start(f32[16]{0:T(128)S(1)} %get-tuple-element.153) | copy-start | bytes 196
  119.4 10.1 %copy-start.55 = (f32[16]{0:T(128)}, f32[16]{0:T(128)S(1)}, u32[]{:S(2)}) copy-start(f32[16]{0:T(128)S(1)} %fusion.94) | copy-start | bytes 196
  120.0 9.4 %copy-start.11 = (f32[16,49,512]{2,1,0:T(8,128)S(1)}, f32[16,49,512]{2,1,0:T(8,128)}, u32[]{:S(2)}) copy-start(f32[16,49,512]{2,1,0:T(8,128)} %get-tuple-element.152) | copy-start | bytes 4816900
  120.1 9.4 %copy-start.93 = (bf16[2,512,2048]{2,1,0:T(8,128)(2,1)S(1)}, bf16[2,512,2048]{2,1,0:T(8,128)(2,1)}, u32[]{:S(2)}) copy-start(bf16[2,512,2048]{2,1,0:T(8,128)(2,1)} %get-tuple-element.30) | copy-start | bytes 12582916
  132.9 10.5 %copy-start.14 = (f32[16,49,512]{2,1,0:T(8,128)}, f32[16,49,512]{2,1,0:T(8,128)S(1)}, u32[]{:S(2)}) copy-start(f32[16,49,512]{2,1,0:T(8,128)S(1)} %get-tuple-element.138) | copy-start | bytes 4816900
  145.3 14.1 %copy-start.19 = (f32[16,49,512]{2,1,0:T(8,128)}, f32[16,49,512]{2,1,0:T(8,128)S(1)}, u32[]{:S(2)}) copy-start(f32[16,49,512]{2,1,0:T(8,128)S(1)} %get-tuple-element.107) | copy-start | bytes 4816900
  160.1 10.6 %copy-start.17 = (f32[16,49,512]{2,1,0:T(8,128)}, f32[16,49,512]{2,1,0:T(8,128)S(1)}, u32[]{:S(2)}) copy-start(f32[16,49,512]{2,1,0:T(8,128)S(1)} %multiply_add_fusion.1) | copy-start | bytes 4816900
  209.0 10.7 %slice-start.4 = ((s8[7340032]{0:T(1024)(128)(4,1)}), s8[4194304]{0:T(1024)(128)(4,1)S(1)}, s32[]{:S(2)}) async-start(s8[7340032]{0:T(1024)(128)(4,1)} %bitcast.305), calls=%async_computation.4 | async-start | bytes 8388608
  (82 other events, 410.9 us)

commit v2 on v0

v2 whole, which is shorter than its diff:
```python
import functools

import jax
import jax.numpy as jnp
from jax import lax
from jax.experimental import pallas as pl
from jax.experimental.pallas import tpu as pltpu
from jax.sharding import PartitionSpec as P

EPS = 1e-6
CHANNEL_AXES = ('tp', 'fsdp')
LAYER_NAMES = ('ln1_g', 'ln1_b', 'w_tok1', 'b_tok1', 'w_tok2', 'ln2_g', 'ln2_b', 'w_ch1', 'b_ch1', 'w_ch2', 'b_ch2')
N0, N1, N2, N3, N4, N5, N6, N7, N8 = range(9)
MESH = pl.DeviceIdType.MESH
BF16 = jnp.bfloat16
F32 = jnp.float32
ORDERS = ((N0, N1, N2), (N1, N2, N0), (N2, N0, N1))


def my_position():
    tp, fsdp = lax.axis_index('tp'), lax.axis_index('fsdp')
    return (lax.rem(fsdp // N2, N2), fsdp // N4, tp), lax.rem(fsdp, N2)


def aligned(value, size):
    return value if isinstance(value, int) else pl.multiple_of(value, size)


def odd(value):
    return value % N2 if isinstance(value, int) else lax.rem(value, N2)


def shifted(coords, bits):
    return tuple(N1 - c if b else c for c, b in zip(coords, bits))


def owner_of(coords, core):
    x, y, z = coords
    return z, y * N4 + x * N2 + core


def device_of(coords, core):
    tp, fsdp = owner_of(coords, core)
    return {'tp': tp, 'fsdp': fsdp}


def unit(dim):
    return tuple(N1 if d == dim else N0 for d in range(N3))


def plus(a, b):
    return tuple((i + j) % N2 for i, j in zip(a, b))


def entry_barrier(coords, core):
    barrier = pltpu.get_barrier_semaphore()
    for dim in range(N3):
        pl.semaphore_signal(barrier, inc=N1, device_id=device_of(shifted(coords, unit(dim)), core), device_id_type=MESH)
    pl.semaphore_signal(barrier, inc=N1, device_id=device_of(coords, N1 - core), device_id_type=MESH)
    pl.semaphore_wait(barrier, N4)


ROW_VEC = dict(b_stem=N0, ln1_g=N1, ln1_b=N3, ln2_g=N5, ln2_b=N7, b_ch2=9, b_ch1=11, lnf_g=19, lnf_b=20, b_head=21, loss=23)
VEC_ROWS = 24
TOK = 56
IMAGES = 16
ROWS = TOK * IMAGES
BAND = 128
BANDS = ROWS // BAND
WIDE = 512
DEEP = 2048
HALF = ROWS // N2
GELU_A = 0.7978845608028654
GELU_B = 0.044715


def by_rows(left, right):
    return lax.dot_general(left, right, (((N1,), (N1,)), ((), ())), preferred_element_type=F32)


def times(left, right):
    return jnp.dot(left, right, preferred_element_type=F32)


def gelu_pair(pre):
    square = pre * pre
    tanh = jnp.tanh(GELU_A * (pre + GELU_B * (square * pre)))
    cdf = 0.5 + 0.5 * tanh
    slope = cdf + (0.5 * pre) * (1.0 - tanh * tanh) * (GELU_A + (3.0 * GELU_A * GELU_B) * square)
    return pre * cdf, slope


def standardize(values):
    centered = values - jnp.mean(values, axis=N1, keepdims=True)
    inv_std = lax.rsqrt(jnp.mean(centered * centered, axis=N1, keepdims=True) + EPS)
    return centered * inv_std, inv_std


def norm_back(grad_out, gain, standard, inv_std):
    grad_std = grad_out * gain
    first = jnp.mean(grad_std, axis=N1, keepdims=True)
    second = jnp.mean(grad_std * standard, axis=N1, keepdims=True)
    return inv_std * (grad_std - first - standard * second)


def row_sum(values):
    return jnp.sum(values, axis=N0, keepdims=True)


DIMS = range(N3)


STEM_W, SMALL, HEAD_W, CHAN1, CHAN2 = N0, N1, N6, (N2, N4), (N3, N5)
GATHER_SPLITS = (((N0, 128), (128, 128), (256, 128)), ((N0, 72), (72, 64), (136, 64)),
                 ((N0, 16), (16, 16), (32, 32)), ((N0, 48), (48, 48), (96, 32)),
                 ((N0, 16), (16, 16), (32, 32)), ((N0, 48), (48, 48), (96, 32)), ((N0, 32), (32, 16), (48, 16)))
GATHERED = len(GATHER_SPLITS)
PACK_ROWS = 200
AT_B1, AT_BT, AT_BH, AT_T1, AT_T2 = 16, 18, 20, 24, 136
VECTORS = (('b_stem', N1), ('ln1_g', N2), ('ln1_b', N2), ('ln2_g', N2), ('ln2_b', N2), ('b_ch2', N2), ('lnf_g', N1), ('lnf_b', N1))
CLASSES_HALF = 500
TOKENS = 49
TOTAL = 256
PATCH = 3072


def forward_kernel(*refs):
    take = iter(refs)

    def grab(count):
        return [next(take) for _ in range(count)]
    patch_hbm, labels, f_stem, f1, f2, f_head = grab(N6)
    vec_in = grab(len(VECTORS))
    i_b1, i_bt, i_bh, i_t1, i_t2 = grab(N5)
    w1_out, w2_out, xa_out, xb_out, patch_out, t1t, t1, t2, bt, vec, gh, hs, d0 = grab(13)
    own_stem, own1, own2, own_head, pack = grab(N5)
    stem_w, small, w1, w2, head_w = grab(N5)
    pin, padded, pbuf, t2t = grab(N4)
    xs = grab(N5)
    v, pre, act, pooled = grab(N4)
    send_sem, recv_sem, load_sem, save_sem = grab(N4)
    coords, core = my_position()
    tp = coords[N2]
    half_images = pin.shape[N0]
    loads = []
    for b in range(half_images):
        copy = pltpu.make_async_copy(patch_hbm.at[tp * half_images + b], pin.at[b], load_sem.at[b])
        copy.start()
        loads.append(copy)

    own_stem[...] = f_stem[...].astype(BF16)
    own1[...] = f1[...].astype(BF16)
    own2[...] = f2[...].astype(BF16)
    own_head[...] = jnp.zeros(own_head.shape, BF16)
    own_head[:, :CLASSES_HALF] = f_head[...].astype(BF16)
    pack[...] = jnp.zeros(pack.shape, F32)
    row = N0
    for ref, (_, num) in zip(vec_in, VECTORS):
        pack[row:row + num, :32] = ref[...]
        row += num
    pack[AT_B1:AT_B1 + N2, :] = i_b1[...]
    pack[AT_BT:AT_BT + N2, :32] = i_bt[...]
    for k in range(N4):
        width = min(BAND, CLASSES_HALF - k * BAND)
        pack[AT_BH + k:AT_BH + k + N1, :width] = i_bh[:, k * BAND:k * BAND + width]
    for layer in range(N2):
        pack[AT_T1 + TOK * layer:AT_T1 + TOK * layer + TOKENS, :32] = i_t1[layer]
        pack[AT_T2 + 32 * layer:AT_T2 + 32 * layer + 32, :TOKENS] = i_t2[layer]
    entry_barrier(coords, core)

    own = [own_stem, pack, own1.at[N0], own2.at[N0], own1.at[N1], own2.at[N1], own_head]

    def block(item, tp, fsdp, lo, num):
        if item == STEM_W:
            return stem_w.at[pl.ds(aligned(fsdp * 384 + lo, 128), num), pl.ds(aligned(tp * 256, 128), 256)]
        if item == SMALL:
            return small.at[tp * N8 + fsdp, pl.ds(lo, num), :]
        if item in CHAN1:
            return w1.at[CHAN1.index(item), pl.ds(aligned(fsdp * 64 + lo, 16), num), pl.ds(aligned(tp * 1024, 128), 1024)]
        if item in CHAN2:
            return w2.at[CHAN2.index(item), pl.ds(aligned((tp * N8 + fsdp) * 128 + lo, 16), num), :]
        return head_w.at[pl.ds(aligned(fsdp * 64 + lo, 16), num), pl.ds(aligned(tp * WIDE, 128), WIDE)]

    def move(item, part, bits, is_own, target, slot):
        lo, num = GATHER_SPLITS[item][part]
        there = block(item, *owner_of(shifted(coords, bits), core), lo, num)
        here = own[item].at[pl.ds(lo, num), :] if is_own else there
        pltpu.make_async_remote_copy(src_ref=here, dst_ref=there, send_sem=send_sem,
                                     recv_sem=recv_sem.at[item, part, slot], device_id=target,
                                     device_id_type=MESH).start()

    def arrival(item, part, bits, from_core, slot):
        lo, num = GATHER_SPLITS[item][part]
        there = block(item, *owner_of(shifted(coords, bits), from_core), lo, num)
        pltpu.make_async_remote_copy(src_ref=there, dst_ref=there, send_sem=send_sem,
                                     recv_sem=recv_sem.at[item, part, slot], device_id=device_of(coords, core),
                                     device_id_type=MESH).wait_recv()

    def pass_on(item, part, bits, level):
        order = ORDERS[part]
        rank = sum(N2 ** i for i in DIMS if bits[order[i]])
        for step in range(level, N3):
            move(item, part, bits, level == N0, device_of(shifted(coords, unit(order[step])), core),
                 N2 ** step - N1 + rank)
        move(item, part, bits, level == N0, device_of(coords, N1 - core), N7 + rank)

    def bits_of(part, rank):
        bits = [N0, N0, N0]
        for i in DIMS:
            bits[ORDERS[part][i]] = (rank >> i) % N2
        return tuple(bits)

    def send_own(item):
        for part in DIMS:
            pass_on(item, part, (N0, N0, N0), N0)

    def forward(item, level):
        for part in DIMS:
            for rank in range(N2 ** level):
                bits = bits_of(part, rank + N2 ** level)
                arrival(item, part, bits, core, N2 ** level - N1 + rank)
                pass_on(item, part, bits, level + N1)

    def finish(item):
        for part in DIMS:
            for rank in range(N8):
                arrival(item, part, bits_of(part, rank), N1 - core, N7 + rank)

    def place_own(item):
        here = own[item]
        block(item, *owner_of(coords, core), N0, here.shape[N0])[...] = here[...]

    saves = []

    def save(src, dst):
        copy = pltpu.make_async_copy(src, dst, save_sem.at[len(saves)])
        copy.start()
        saves.append((src, dst))

    early = (STEM_W, SMALL)
    for item in early:
        send_own(item)
    send_own(CHAN1[N0])
    for item in range(GATHERED):
        place_own(item)
    padded[...] = jnp.zeros(padded.shape, F32)
    for item in early:
        forward(item, N0)
    send_own(CHAN2[N0])

    def pad_patches(q):
        for i in range(N2):
            padded[i * TOK:i * TOK + TOKENS, :] = pin[N2 * q + i].astype(F32)
        pbuf[pl.ds(aligned(q * N2 * TOK, 16), N2 * TOK), :] = padded[...].astype(BF16)
    for copy in loads:
        copy.wait()
    for item in early:
        forward(item, N1)
    send_own(CHAN1[N1])
    pl.loop(N0, N4)(pad_patches)
    for item in early:
        forward(item, N2)
    send_own(CHAN2[N1])
    send_own(HEAD_W)
    pl.loop(N4, N8)(pad_patches)
    save(pbuf, patch_out)
    forward(CHAN1[N0], N0)
    for item in early:
        finish(item)

    lane32 = lax.broadcasted_iota(jnp.int32, (N1, BAND), N1) // 32

    def lay_out(q, lo, num):
        total = None
        for i in range(N4):
            piece = small[N4 * q + i, lo:lo + num, :]
            piece = jnp.where(lane32 == i, pltpu.roll(piece, 32 * i, N1) if i else piece, 0.0)
            total = piece if total is None else total + piece
        return total
    vec[...] = jnp.zeros(vec.shape, F32)
    rows_first, lnf = ROW_VEC['b_ch1'], ROW_VEC['lnf_g']
    for q in range(N4):
        cols = slice(q * BAND, q * BAND + BAND)
        found = lay_out(q, N0, 16)
        vec[:rows_first, cols] = found[:rows_first]
        vec[lnf:lnf + N2, cols] = found[rows_first:rows_first + N2]
        for layer in range(N2):
            for j in range(N4):
                at = rows_first + N4 * layer + j
                vec[at:at + N1, cols] = small[N4 * j + q, AT_B1 + layer:AT_B1 + layer + N1, :]
        for z in range(N2):
            at = ROW_VEC['b_head'] + z
            vec[at:at + N1, cols] = small[N8 * z, AT_BH + q:AT_BH + q + N1, :]
    for q in range(N2):
        cols = slice(q * BAND, q * BAND + BAND)
        turned = lay_out(q, AT_B1, N8).T
        for layer in range(N2):
            column = AT_BT - AT_B1 + layer
            bt[layer, cols, :] = turned[:, column:column + N1]
            found = lay_out(q, AT_T1 + TOK * layer, TOK)
            t1[layer, :, cols] = found.astype(BF16)
            t1t[layer, cols, :] = found.T.astype(BF16)
            rows = jnp.concatenate([small[N4 * q + i, AT_T2 + 32 * layer:AT_T2 + 32 * layer + 32, :] for i in range(N4)],
                                   axis=N0)
            t2[layer, cols, :] = rows[:, :TOK].astype(BF16)
            t2t[layer, :, cols] = rows.T[:TOK].astype(BF16)

    def vector(name, at=N0):
        return vec[pl.ds(ROW_VEC[name] + at, N1), :]

    tasks = [lambda: forward(CHAN2[N0], N0), lambda: forward(CHAN1[N0], N1)]

    @pl.loop(N0, N2)
    def _(h):
        rows = pl.ds(aligned(h * HALF, HALF), HALF)
        xs[N0][rows, :] = times(pbuf[rows, :], stem_w[...]) + vector('b_stem')
        for k, task in enumerate(tasks):
            pl.when(h == k)(task)
    save(xs[N0], xa_out.at[N0])

    def token_mix(layer, tasks):
        source, target = xs[N2 * layer], xs[N2 * layer + N1]
        gain, shift = vector('ln1_g', layer), vector('ln1_b', layer)

        @pl.loop(N0, IMAGES)
        def _(b):
            rows = pl.ds(aligned(b * TOK, N8), TOK)
            here = source[rows, :]
            norm = (standardize(here)[N0] * gain + shift).astype(BF16)
            hidden = jax.nn.gelu(times(t1t[layer], norm) + bt[layer]).astype(BF16)
            target[rows, :] = here + times(t2t[layer], hidden)
            for k, task in tasks:
                pl.when(b == k)(task)

    def channel_mix(layer, tasks):
        source, target = xs[N2 * layer + N1], xs[N2 * layer + N2]
        gain, shift = vector('ln2_g', layer), vector('ln2_b', layer)

        @pl.loop(N0, BANDS)
        def _(i):
            rows = pl.ds(aligned(i * BAND, BAND), BAND)
            here = source[rows, :]
            v[rows, :] = (standardize(here)[N0] * gain + shift).astype(BF16)
            target[rows, :] = here + vector('b_ch2', layer)

        @pl.loop(N0, N4)
        def _(j):
            cols = pl.ds(aligned(j * WIDE, WIDE), WIDE)
            bias = vector('b_ch1', N4 * layer + j)
            for half in range(N2):
                rows = pl.ds(half * HALF, HALF)
                pre[...] = times(v[rows, :], w1[layer, :, cols])

                @pl.loop(N0, HALF // 32)
                def _(i):
                    part = pl.ds(aligned(i * 32, 32), 32)
                    act[part, :] = jax.nn.gelu(pre[part, :] + bias).astype(BF16)
                target[rows, :] = target[rows, :] + times(act[...], w2[layer, cols, :])
            for k, task in tasks:
                pl.when(j == k)(task)

    token_mix(N0, [(N1, lambda: forward(CHAN2[N0], N1)), (N4, lambda: forward(CHAN1[N0], N2)),
                  (N6, lambda: forward(CHAN2[N0], N2)), (N8, lambda: forward(CHAN1[N1], N0)),
                  (10, lambda: forward(CHAN2[N1], N0)), (12, lambda: forward(HEAD_W, N0)),
                  (14, lambda: forward(CHAN1[N1], N1))])
    save(xs[N1], xb_out.at[N0])
    finish(CHAN1[N0])
    finish(CHAN2[N0])
    save(w1.at[N0], w1_out.at[N0])
    save(w2.at[N0], w2_out.at[N0])
    channel_mix(N0, [(N0, lambda: forward(CHAN2[N1], N1)), (N1, lambda: forward(HEAD_W, N1)),
                    (N2, lambda: forward(CHAN1[N1], N2)), (N3, lambda: forward(CHAN2[N1], N2))])
    save(xs[N2], xa_out.at[N1])
    token_mix(N1, [(N0, lambda: forward(HEAD_W, N2))])
    save(xs[N3], xb_out.at[N1])
    for item in (CHAN1[N1], CHAN2[N1], HEAD_W):
        finish(item)
    save(w1.at[N1], w1_out.at[N1])
    save(w2.at[N1], w2_out.at[N1])
    channel_mix(N1, [])

    real_row = lax.broadcasted_iota(jnp.int32, (TOK, N1), N0) < TOKENS

    @pl.loop(N0, IMAGES)
    def _(b):
        here = xs[N4][pl.ds(aligned(b * TOK, N8), TOK), :]
        pooled[pl.ds(b, N1), :] = row_sum(jnp.where(real_row, here, 0.0)) * (1.0 / TOKENS)
    gain = vector('lnf_g')
    standard, inv_std = standardize(pooled[...])
    norm = standard * gain + vector('lnf_b')
    norm_bf = norm.astype(BF16)
    lane = lax.broadcasted_iota(jnp.int32, (IMAGES, WIDE), N1)
    real = lane < CLASSES_HALF
    logits = [times(norm_bf, head_w[:, z * WIDE:z * WIDE + WIDE]) + vector('b_head', z) for z in range(N2)]
    row_max = jnp.maximum(*[jnp.max(jnp.where(real, l, -jnp.inf), axis=N1, keepdims=True) for l in logits])
    exps = [jnp.where(real, jnp.exp(jnp.where(real, l, row_max) - row_max), 0.0) for l in logits]
    sums = jnp.sum(exps[N0], axis=N1, keepdims=True) + jnp.sum(exps[N1], axis=N1, keepdims=True)
    mine = labels[pl.ds(aligned(tp * IMAGES, N8), IMAGES), :]
    hits = [jnp.logical_and(lane + z * CLASSES_HALF == mine, real) for z in range(N2)]
    picked = sum(jnp.sum(jnp.where(hit, l, 0.0), axis=N1, keepdims=True) for hit, l in zip(hits, logits))
    losses = row_max + jnp.log(sums) - picked
    hs[...] = jnp.zeros(hs.shape, F32)
    turned = norm.T.astype(BF16)
    back = None
    for z in range(N2):
        d_logits = (exps[z] / sums - hits[z].astype(F32)) * (1.0 / TOTAL)
        d_logits_bf = d_logits.astype(BF16)
        gh[:, z * WIDE:z * WIDE + WIDE] = times(turned, d_logits_bf)
        at = ROW_VEC['b_head'] + z
        hs[at:at + N1, :] = row_sum(d_logits)
        piece = by_rows(d_logits_bf, head_w[:, z * WIDE:z * WIDE + WIDE])
        back = piece if back is None else back + piece
    hs[lnf:lnf + N1, :] = row_sum(back * standard)
    hs[lnf + N1:lnf + N2, :] = row_sum(back)
    at = ROW_VEC['loss']
    hs[at:at + N1, :] = jnp.broadcast_to(row_sum(losses) * (1.0 / TOTAL), (N1, WIDE))
    d0[...] = norm_back(back, gain, standard, inv_std) * (1.0 / TOKENS)

    for k, (src, dst) in enumerate(saves):
        pltpu.make_async_copy(src, dst, save_sem.at[k]).wait()
    for item in range(GATHERED):
        for part in DIMS:
            lo, num = GATHER_SPLITS[item][part]
            here = own[item].at[pl.ds(lo, num), :]
            for _ in range(15):
                pltpu.make_async_remote_copy(src_ref=here, dst_ref=here, send_sem=send_sem,
                                             recv_sem=recv_sem.at[item, part, N0], device_id=device_of(coords, core),
                                             device_id_type=MESH).wait_send()


def forward_all(*operands):
    any_spec, vmem = pl.BlockSpec(memory_space=pl.ANY), pl.BlockSpec(memory_space=pltpu.VMEM)
    shape = jax.ShapeDtypeStruct
    plane = (ROWS, WIDE)
    outs = [shape((N2, WIDE, DEEP), BF16), shape((N2, DEEP, WIDE), BF16), shape((N2,) + plane, F32),
            shape((N2,) + plane, F32), shape((ROWS, PATCH), BF16), shape((N2, 256, TOK), BF16),
            shape((N2, TOK, 256), BF16), shape((N2, 256, TOK), BF16), shape((N2, 256, N1), F32),
            shape((VEC_ROWS, WIDE), F32), shape((WIDE, N2 * WIDE), F32), shape((VEC_ROWS, WIDE), F32),
            shape((IMAGES, WIDE), F32)]
    dma = pltpu.SemaphoreType.DMA
    return pl.pallas_call(
        forward_kernel, out_shape=outs, in_specs=[any_spec] + [vmem] * (len(operands) - N1),
        out_specs=[any_spec] * N5 + [vmem] * N8,
        scratch_shapes=[
            pltpu.VMEM((384, 256), BF16), pltpu.VMEM((N2, 64, 1024), BF16), pltpu.VMEM((N2, 128, WIDE), BF16),
            pltpu.VMEM((64, WIDE), BF16), pltpu.VMEM((PACK_ROWS, BAND), F32),
            pltpu.VMEM((PATCH, WIDE), BF16), pltpu.VMEM((16, PACK_ROWS, BAND), F32), pltpu.VMEM((N2, WIDE, DEEP), BF16),
            pltpu.VMEM((N2, DEEP, WIDE), BF16), pltpu.VMEM((WIDE, N2 * WIDE), BF16),
            pltpu.VMEM((IMAGES, TOKENS, PATCH), BF16), pltpu.VMEM((N2 * TOK, PATCH), F32), pltpu.VMEM((ROWS, PATCH), BF16),
            pltpu.VMEM((N2, TOK, 256), BF16)] + [pltpu.VMEM(plane, F32)] * N5 + [
            pltpu.VMEM(plane, BF16), pltpu.VMEM((HALF, WIDE), F32), pltpu.VMEM((HALF, WIDE), BF16),
            pltpu.VMEM((IMAGES, WIDE), F32),
            dma, dma((GATHERED, N3, 15)), dma((IMAGES,)), dma((9,))],
        compiler_params=pltpu.CompilerParams(collective_id=N0, has_side_effects=True, vmem_limit_bytes=67043328),
        cost_estimate=pl.CostEstimate(flops=10 ** 9, bytes_accessed=25 * 10 ** N6, transcendentals=N0),
        name='forward')(*operands)


HEAD, CH1, CH2, STEM = N0, (N1, N3), (N2, N4), N5
ITEM_SHAPES = ((64, 512), (64, 1024), (512, 128), (64, 1024), (512, 128), (256, 384))
ITEM_SPLITS = tuple(tuple((lo, hi - lo) for lo, hi in zip((N0,) + cut, cut + (shape[N0],)))
                    for shape, cut in zip(ITEM_SHAPES, ((24, 48), (24, 48), (176, 344), (24, 48), (176, 344), (88, 176))))
ITEMS = len(ITEM_SHAPES)


def backward_kernel(*refs):
    take = iter(refs)

    def grab(count):
        return [next(take) for _ in range(count)]
    w1_hbm, w2_hbm, t1t, t1, t2, bt, vec, xa_hbm, xb_hbm, d0, patch_hbm, gh_hbm, hs = grab(13)
    o_stem, o1, o2, oh, osum, otok = grab(N6)
    mine, peer = grab(ITEMS), grab(ITEMS)
    boxes = [[grab(N3) for _ in DIMS] for _ in range(ITEMS)]
    w1, w2, xa, xb, grad, acc, v, vt, dout, dout_t, pre, dact, act, dpre, g1, g2, pbuf, gs = grab(18)
    tacc1, tacc2, bacc, sbox, tbox = grab(N5)
    send_sem, hop_sem, peer_sem, pair_sem, load_sem, red_send, red_recv = grab(N7)
    coords, core = my_position()
    other = N1 - core
    entry_barrier(coords, core)
    partner = device_of(coords, other)
    pending = []

    def start(src, dst, sem, device, sent=None):
        copy = pltpu.make_async_remote_copy(src_ref=src, dst_ref=dst, send_sem=send_sem if sent is None else sent,
                                            recv_sem=sem, device_id=device, device_id_type=MESH)
        copy.start()
        return copy

    def arrived(dst, sem):
        pltpu.make_async_remote_copy(src_ref=dst, dst_ref=dst, send_sem=send_sem, recv_sem=sem,
                                     device_id=partner, device_id_type=MESH).wait_recv()

    def left(src, sent):
        pltpu.make_async_remote_copy(src_ref=src, dst_ref=src, send_sem=sent, recv_sem=pair_sem.at[N0],
                                     device_id=partner, device_id_type=MESH).wait_send()

    def view(ref, item, part, select):
        lo, num = ITEM_SPLITS[item][part]
        x, y, z = select
        return ref.at[z, y, x, pl.ds(lo, num), :]

    def phase_source(item, part, phase):
        order = ORDERS[part]
        select = [pl.ds(N0, N2)] * N3
        for dim in order[:phase]:
            select[dim] = coords[dim]
        select[order[phase]] = N1 - coords[order[phase]]
        return view(mine[item], item, part, select)

    def phase_send(item, phase):
        for part in DIMS:
            start(phase_source(item, part, phase), boxes[item][part][phase], hop_sem.at[item, part, phase],
                  device_of(shifted(coords, unit(ORDERS[part][phase])), core))

    def phase_take(item, phase, final=None):
        for part in DIMS:
            order = ORDERS[part]
            box = boxes[item][part][phase]
            arrived(box, hop_sem.at[item, part, phase])
            rest = [dim for dim in (N2, N1, N0) if dim in order[phase + N1:]]
            for sub in range(N2 ** len(rest)):
                bits = [(sub >> place) % N2 for place in range(len(rest))]
                select = list(coords)
                for dim, bit in zip(rest, bits):
                    select[dim] = bit
                here = view(mine[item], item, part, select)
                total = here[...] + (box.at[tuple(bits)] if bits else box)[...]
                if final is None:
                    here[...] = total
                else:
                    lo, num = ITEM_SPLITS[item][part]
                    final[pl.ds(lo, num), :] = total

    def add_peer(item):
        @pl.loop(N0, N8)
        def _(i):
            at = (i // N4, odd(i // N2), odd(i))
            mine[item][at] = mine[item][at] + peer[item][at]

    def advance(items, phase, finals=None):
        for index, item in enumerate(items):
            phase_take(item, phase, None if finals is None else finals[index])
            if phase < N2:
                phase_send(item, phase + N1)

    def reduce_send(parts, stage):
        device = partner if stage == N0 else device_of(shifted(coords, unit(stage - N1)), core)
        for ref, box, slot in parts:
            start(ref, box.at[stage], red_recv.at[slot, stage], device, red_send.at[slot])

    def reduce_take(parts, stage):
        for ref, box, slot in parts:
            arrived(box.at[stage], red_recv.at[slot, stage])
            left(ref, red_send.at[slot])
            ref[...] = ref[...] + box[stage]

    def reduce_step(parts, stage):
        reduce_take(parts, stage)
        if stage < N3:
            reduce_send(parts, stage + N1)

    def load(src, dst, slot):
        copy = pltpu.make_async_copy(src, dst, load_sem.at[slot])
        copy.start()
        return copy

    def head_view(f):
        return gh_hbm.at[pl.ds(aligned(f * 64, 64), 64), :]
    first = [load(w1_hbm.at[N1], w1, N0), load(w2_hbm.at[N1], w2, N1), load(xb_hbm.at[N1], xb, N2)]
    xa_copy = load(xa_hbm.at[N1], xa, N4)
    heads = []
    for y in range(N2):
        for x in range(N2):
            for z in range(N2):
                slot = y * N4 + x * N2 + z
                pending.append(start(head_view(y * N4 + x * N2 + other).at[:, pl.ds(z * WIDE, WIDE)],
                                     peer[HEAD].at[z, y, x], pair_sem.at[slot], partner))
                heads.append(load(head_view(y * N4 + x * N2 + core).at[:, pl.ds(z * WIDE, WIDE)],
                                  mine[HEAD].at[z, y, x], N5 + slot))
    osum[...] = hs[...]
    real_row = lax.broadcasted_iota(jnp.int32, (TOK, N1), N0) < TOKENS

    @pl.loop(N0, IMAGES)
    def _(b):
        grad[pl.ds(aligned(b * TOK, N8), TOK), :] = jnp.where(real_row, d0[pl.ds(b, N1), :], 0.0)

    def head_start():
        for y in range(N2):
            for x in range(N2):
                for z in range(N2):
                    slot = y * N4 + x * N2 + z
                    heads[slot].wait()
                    arrived(peer[HEAD].at[z, y, x], pair_sem.at[slot])
        add_peer(HEAD)
        phase_send(HEAD, N0)

    def add_row(name, at, values):
        row = pl.ds(ROW_VEC[name] + at, N1)
        osum[row, :] = osum[row, :] + values

    def chunk_moves(layer, j):
        z, y = j // N2, odd(j)
        moves = [(g1.at[:, :, other], peer[CH1[layer]].at[z, :, :, :, pl.ds(aligned(y * WIDE, WIDE), WIDE)])]
        for x in range(N2):
            moves.append((g2.at[:, pl.ds(aligned((N2 * x + other) * BAND, BAND), BAND)],
                          peer[CH2[layer]].at[z, y, x]))
        return [(src, dst, peer_sem.at[layer, k, j]) for k, (src, dst) in enumerate(moves)]

    def channel_back(layer, steps):
        gain, shift = vec[pl.ds(ROW_VEC['ln2_g'] + layer, N1), :], vec[pl.ds(ROW_VEC['ln2_b'] + layer, N1), :]

        @pl.loop(N0, BANDS)
        def _(i):
            rows = pl.ds(aligned(i * BAND, BAND), BAND)
            standard, _ = standardize(xb[rows, :])
            norm = standard * gain + shift
            v[rows, :] = norm.astype(BF16)
            vt[:, rows] = norm.T.astype(BF16)
            here = grad[rows, :]
            dout[rows, :] = here.astype(BF16)
            dout_t[:, rows] = here.T.astype(BF16)
            add_row('b_ch2', layer, row_sum(here))
            acc[rows, :] = jnp.zeros((BAND, WIDE), F32)

        @pl.loop(N0, N4)
        def _(j):
            cols = pl.ds(aligned(j * WIDE, WIDE), WIDE)
            bias = vec[pl.ds(ROW_VEC['b_ch1'] + N4 * layer + j, N1), :]
            bacc[...] = jnp.zeros(bacc.shape, F32)
            for half in range(N2):
                rows = pl.ds(half * HALF, HALF)
                pre[...] = times(v[rows, :], w1[:, cols])
                dact[...] = by_rows(dout[rows, :], w2[cols, :])

                @pl.loop(N0, HALF // 32)
                def _(i):
                    small = pl.ds(aligned(i * 32, 32), 32)
                    value, slope = gelu_pair(pre[small, :] + bias)
                    change = dact[small, :] * slope
                    where = pl.ds(aligned(half * HALF + i * 32, 32), 32)
                    act[where, :] = value.astype(BF16)
                    dpre[where, :] = change.astype(BF16)
                    bacc[...] = bacc[...] + jnp.sum(change.reshape(N4, N8, WIDE), axis=N0)
                acc[rows, :] = acc[rows, :] + by_rows(dpre[rows, :], w1[:, cols])
            add_row('b_ch1', N4 * layer + j, row_sum(bacc[...]))

            @pl.when(j > N0)
            def _():
                for src, _, _ in chunk_moves(layer, j):
                    left(src, pair_sem.at[N8])
            g1[...] = times(vt[...], dpre[...]).reshape(g1.shape)
            g2[...] = times(dout_t[...], act[...])
            for src, dst, sem in chunk_moves(layer, j):
                start(src, dst, sem, partner, pair_sem.at[N8])
            z, y = j // N2, odd(j)
            mine[CH1[layer]][z, :, :, :, pl.ds(aligned(y * WIDE, WIDE), WIDE)] = g1[:, :, core]
            for x in range(N2):
                mine[CH2[layer]][z, y, x] = g2[:, pl.ds(aligned((N2 * x + core) * BAND, BAND), BAND)]
            for k, step in enumerate(steps):
                pl.when(j == k)(step)
        for src, _, _ in chunk_moves(layer, N3):
            left(src, pair_sem.at[N8])
        for j in range(N4):
            for _, dst, sem in chunk_moves(layer, j):
                arrived(dst, sem)
        for item in (CH1[layer], CH2[layer]):
            add_peer(item)
            phase_send(item, N0)

        @pl.loop(N0, BANDS)
        def _(i):
            rows = pl.ds(aligned(i * BAND, BAND), BAND)
            standard, inv_std = standardize(xb[rows, :])
            here = acc[rows, :]
            add_row('ln2_g', layer, row_sum(here * standard))
            add_row('ln2_b', layer, row_sum(here))
            grad[rows, :] = grad[rows, :] + norm_back(here, gain, standard, inv_std)

    def token_back(layer, steps):
        gain, shift = vec[pl.ds(ROW_VEC['ln1_g'] + layer, N1), :], vec[pl.ds(ROW_VEC['ln1_b'] + layer, N1), :]
        tacc1[...] = jnp.zeros(tacc1.shape, F32)
        tacc2[...] = jnp.zeros(tacc2.shape, F32)
        pre256, change256 = pre.at[pl.ds(N0, 256), :], dact.at[pl.ds(N0, 256), :]

        @pl.loop(N0, IMAGES)
        def _(b):
            rows = pl.ds(aligned(b * TOK, N8), TOK)
            standard, inv_std = standardize(xa[rows, :])
            norm = (standard * gain + shift).astype(BF16)
            here = grad[rows, :]
            here_bf = here.astype(BF16)
            value, slope = gelu_pair(times(t1t[layer], norm) + bt[layer])
            change = times(t2[layer], here_bf) * slope
            change_bf = change.astype(BF16)
            total = change[:, :BAND]
            for k in range(N1, N4):
                total = total + change[:, k * BAND:(k + N1) * BAND]
            tacc1[:, BAND:] = tacc1[:, BAND:] + total
            tacc1[:, :TOK] = tacc1[:, :TOK] + by_rows(change_bf, norm)
            tacc2[:, :TOK] = tacc2[:, :TOK] + by_rows(value.astype(BF16), here_bf)
            d_norm = times(t1[layer], change_bf)
            add_row('ln1_g', layer, row_sum(d_norm * standard))
            add_row('ln1_b', layer, row_sum(d_norm))
            grad[rows, :] = here + norm_back(d_norm, gain, standard, inv_std)
            for k, step in steps:
                pl.when(b == k)(step)
        lane = lax.broadcasted_iota(jnp.int32, (256, BAND), N1)
        bias_grad = jnp.sum(tacc1[:, BAND:], axis=N1, keepdims=True)
        otok[layer] = (jnp.where(lane < TOK, tacc1[:, :BAND], 0.0)
                       + pltpu.roll(jnp.where(lane < TOK, tacc2[...], 0.0), 64, N1)
                       + jnp.where(lane == BAND - N8, bias_grad, 0.0))

    late = [(otok.at[N1], tbox.at[N1], N1)]
    final = [(otok.at[N0], tbox.at[N0], N0), (osum, sbox, N2)]
    layer1, layer0 = (CH1[N1], CH2[N1]), (CH1[N0], CH2[N0])

    for copy in first:
        copy.wait()
    channel_back(N1, [head_start, lambda: advance([HEAD], N0), lambda: advance([HEAD], N1),
                     lambda: advance([HEAD], N2, [oh])])
    again = [load(w1_hbm.at[N0], w1, N0), load(w2_hbm.at[N0], w2, N1), load(xb_hbm.at[N0], xb, N2)]
    xa_copy.wait()
    token_back(N1, [(11, lambda: advance(layer1, N0))])
    reduce_send(late, N0)
    xa_copy = load(xa_hbm.at[N0], xa, N4)
    for copy in again:
        copy.wait()

    def second():
        advance(layer1, N1)
        reduce_step(late, N1)

    def third():
        advance(layer1, N2, [o1.at[N1], o2.at[N1]])
        reduce_step(late, N2)
    channel_back(N0, [lambda: reduce_step(late, N0), second, third, lambda: reduce_step(late, N3)])
    xa_copy.wait()
    token_back(N0, [(11, lambda: advance(layer0, N0))])

    @pl.loop(N0, BANDS)
    def _(i):
        rows = pl.ds(aligned(i * BAND, BAND), BAND)
        here = grad[rows, :]
        dout_t[:, rows] = here.T.astype(BF16)
        add_row('b_stem', N0, row_sum(here))
    reduce_send(final, N0)

    def patch_load(k):
        f = (k % N4) * N2 + (other if k < N4 else core)
        return load(patch_hbm.at[:, pl.ds(aligned(f * 384, BAND), 384)], pbuf.at[k % N2], k % N2)
    copies = {N0: patch_load(N0)}
    for k in range(N8):
        if k < N7:
            copies[k + N1] = patch_load(k + N1)
        copies[k].wait()
        y, x = (k % N4) // N2, k % N2
        result = times(dout_t[...], pbuf[k % N2]).reshape(N2, 256, 384)
        if k < N4:
            if k > N0:
                left(gs, pair_sem.at[N8])
            gs[...] = result
            start(gs, peer[STEM].at[:, y, x], pair_sem.at[k], partner, pair_sem.at[N8])
        else:
            mine[STEM][:, y, x] = result
        if k == N3:
            left(gs, pair_sem.at[N8])
            reduce_step(final, N0)
        if k == N5:
            advance(layer0, N1)
    for k in range(N4):
        arrived(peer[STEM].at[:, k // N2, k % N2], pair_sem.at[k])
    add_peer(STEM)
    phase_send(STEM, N0)
    reduce_step(final, N1)
    advance(layer0, N2, [o1.at[N0], o2.at[N0]])
    reduce_step(final, N2)
    advance([STEM], N0)
    reduce_step(final, N3)
    advance([STEM], N1)
    advance([STEM], N2, [o_stem])
    for copy in pending:
        copy.wait_send()
    for item in range(ITEMS):
        for part in DIMS:
            for phase in DIMS:
                left(phase_source(item, part, phase), send_sem)


def backward_all(*operands):
    any_spec, vmem = pl.BlockSpec(memory_space=pl.ANY), pl.BlockSpec(memory_space=pltpu.VMEM)
    boxes = [pltpu.VMEM((N2,) * (N2 - phase) + (ITEM_SPLITS[item][part][N1], ITEM_SHAPES[item][N1]), F32)
             for item in range(ITEMS) for part in DIMS for phase in DIMS]
    slots = [pltpu.VMEM((N2, N2, N2) + shape, F32) for shape in ITEM_SHAPES]
    plane = pltpu.VMEM((ROWS, WIDE), F32)
    plane_bf, turned_bf = pltpu.VMEM((ROWS, WIDE), BF16), pltpu.VMEM((WIDE, ROWS), BF16)
    half = pltpu.VMEM((HALF, WIDE), F32)
    dma = pltpu.SemaphoreType.DMA
    outs = ((256, 384), (N2, 64, 1024), (N2, 512, 128), (64, 512), (VEC_ROWS, WIDE), (N2, 256, 128))
    return pl.pallas_call(
        backward_kernel, out_shape=[jax.ShapeDtypeStruct(s, F32) for s in outs],
        in_specs=[any_spec] * N2 + [vmem] * N5 + [any_spec] * N2 + [vmem] + [any_spec] * N2 + [vmem], out_specs=[vmem] * len(outs),
        scratch_shapes=slots + slots + boxes + [
            pltpu.VMEM((WIDE, DEEP), BF16), pltpu.VMEM((DEEP, WIDE), BF16), plane, plane, plane, plane,
            plane_bf, turned_bf, plane_bf, turned_bf, half, half, plane_bf, plane_bf,
            pltpu.VMEM((N2, N2, N2, 64, WIDE), F32), pltpu.VMEM((WIDE, WIDE), F32),
            pltpu.VMEM((N2, ROWS, 384), BF16), pltpu.VMEM((N2, 256, 384), F32),
            pltpu.VMEM((256, 256), F32), pltpu.VMEM((256, 128), F32), pltpu.VMEM((N8, WIDE), F32),
            pltpu.VMEM((N4, VEC_ROWS, WIDE), F32), pltpu.VMEM((N2, N4, 256, 128), F32),
            dma, dma((ITEMS, N3, N3)), dma((N2, N3, N4)), dma((9,)), dma((13,)), dma((N3,)), dma((N3, N4))],
        compiler_params=pltpu.CompilerParams(collective_id=N1, has_side_effects=True, vmem_limit_bytes=67043328),
        cost_estimate=pl.CostEstimate(flops=10 ** 9, bytes_accessed=50 * 10 ** N6, transcendentals=N0),
        name='backward')(*operands)


def weight_specs():
    vec_spec = P(CHANNEL_AXES)
    layer_vec = P(None, CHANNEL_AXES)
    return (P('fsdp', 'tp'), vec_spec, layer_vec, layer_vec, P(None, None, 'fsdp'), P(None, 'fsdp'),
            P(None, 'fsdp', None), layer_vec, layer_vec, P(None, 'fsdp', 'tp'), layer_vec,
            P(None, CHANNEL_AXES, None), layer_vec, vec_spec, vec_spec, P('fsdp', 'tp'), P('tp'))


def solution(mesh):
    def step(patches, labels, w_stem, b_stem, ln1_g, ln1_b, w_tok1, b_tok1, w_tok2,
             ln2_g, ln2_b, w_ch1, b_ch1, w_ch2, b_ch2, lnf_g, lnf_b, w_head, b_head):
        def flat(values):
            return values.reshape(N1, -N1)
        tp, fsdp = lax.axis_index('tp'), lax.axis_index('fsdp')
        w1, w2, xa, xb, padded, t1t, t1, t2, bt, vec, gh, hs, d0 = forward_all(
            patches, labels.reshape(-N1, N1), w_stem, w_ch1, w_ch2, w_head, flat(b_stem), ln1_g, ln1_b, ln2_g, ln2_b,
            b_ch2, flat(lnf_g), flat(lnf_b), b_ch1, b_tok1, flat(b_head), w_tok1, w_tok2)
        o_stem, o1, o2, oh, osum, otok = backward_all(w1, w2, t1t, t1, t2, bt, vec, xa, xb, d0, padded, gh, hs)
        tokens = TOKENS
        owner = tp * N8 + fsdp
        lanes = lax.dynamic_slice_in_dim(osum, owner * 32, 32, N1)
        found = {name: lanes[ROW_VEC[name]:ROW_VEC[name] + num].reshape((num, 32) if num == N2 else (32,))
                 for name, num in VECTORS}
        deep = osum[ROW_VEC['b_ch1']:ROW_VEC['lnf_g']].reshape(N2, DEEP)
        found['b_ch1'] = lax.dynamic_slice_in_dim(deep, owner * 128, 128, N1)
        found['b_head'] = lax.dynamic_slice_in_dim(osum, ROW_VEC['b_head'] + tp, N1, N0)[N0, :500]
        tok_rows = lax.dynamic_slice_in_dim(otok, fsdp * 32, 32, N1)
        found['w_tok1'] = tok_rows[:, :, :tokens].swapaxes(N1, N2)
        found['w_tok2'] = tok_rows[:, :, 64:64 + tokens]
        found['b_tok1'] = tok_rows[:, :, BAND - N8]
        found['w_ch1'], found['w_ch2'] = o1, o2.swapaxes(N1, N2)
        return tuple([osum[ROW_VEC['loss'], N0], o_stem.T, found['b_stem']] + [found[name] for name in LAYER_NAMES]
                     + [found['lnf_g'], found['lnf_b'], oh[:, :500], found['b_head']])

    specs = weight_specs()
    return jax.shard_map(step, mesh=mesh, in_specs=(P('fsdp', None, None), P('fsdp')) + specs,
                         out_specs=(P(),) + specs, check_vma=False)
```

time: 963 us -> 276 us (0.29); the launches traced: 952 us -> 275 us
  waiting for transfers between devices: 439 us -> 0 us
  blocking collectives: 253 us -> 0 us
  Pallas kernels: 0 us -> 244 us
  matrix products: 162 us -> 0 us
  other arithmetic: 55.9 us -> 0 us
  between operations: 19.3 us -> 0.7 us
    reduce_scatter x15 -> x0, waiting for transfers between devices: 349 us -> none  [the longest x10 245 us: sum_to_piece(): lax.psum_scatter(grad_full, 'fsdp', scatter_dimension=axis, tiled=True)]
    pallas_call x0 -> x2, Pallas kernels: none -> 244 us  [the longest x1 152 us: backward_all(): pl.pallas_call(backward_kernel, out_shape=[jax.ShapeDtypeStruct(s, F32) f...]
    dot_general x29 -> x0, matrix products: 162 us -> none  [product(): return jnp.einsum(form, left, right, preferred_element_type=jnp.float32)]
    psum x13 -> x0, blocking collectives: 119 us -> none  [the longest x5 41.9 us: norm_backward(): moments = lax.psum(moments, 'tp') / width]
    all_gather x14 -> x0, blocking collectives: 116 us -> none  [the longest x7 61.8 us: gather_vector(): return lax.all_gather(values, 'fsdp', axis=values.ndim - 1, tiled=True)]
    all_gather x8 -> x0, waiting for transfers between devices: 88.4 us -> none  [the longest x2 39.4 us: step(): lax.all_gather(normed2.astype(jnp.bfloat16), 'tp', axis=2, tiled=True)]
    reduce_sum x15 -> x0, other arithmetic: 24.9 us -> none  [the longest x6 17.1 us: lead_sum(): return jnp.sum(values.reshape(-1, values.shape[-1]), axis=0)]
    convert_element_type x11 -> x0, other arithmetic: 14.3 us -> none  [the longest x2 5.29 us: step(): d_mid_bf = d_mid.astype(jnp.bfloat16)]
  transfers between devices with their start and end apart: 23 -> 0, of which waited for: 18 -> 0; matrix products, arithmetic and copies ran while one was open for 16% -> 0% of each run, Pallas kernels for 0% -> 0%
where the time goes in v2:
time: 276 us; the launch traced here: 275 us
  Pallas kernels  244 us (88%)
  local copies, waits for them, and re-layouts  30.7 us (11%)
    pallas_call x1, Pallas kernels, backward_all(): pl.pallas_call(backward_kernel, out_shape=[jax.ShapeDtypeStruct(s, F32) f...  152 us
    pallas_call x1, Pallas kernels, forward_all(): pl.pallas_call(forward_kernel, out_shape=outs, in_specs=[any_spec] + [vme...  91.5 us
    unnamed x10, local copies, waits for them, and re-layouts  20.3 us

profile of v2, /device:TPU:0, one launch (start us, length us, event | category | flops | bytes accessed | tf_op | source)
XLA Modules:
  0.0 275.2 jit_solution(11813887269629134901)
XLA Ops:
  0.7 0.0 copy-start
  0.7 0.0 copy-start.1
  0.7 12.2 %copy.42.refs_0_ = bf16[32,49,3072]{2,1,0:T(8,128)(2,1)} copy(bf16[32,49,3072]{2,0,1:T(8,128)(2,1)} %param.19) | data formatting | bytes 19267584 | tf_op args[0]
  12.9 0.0 copy-done
  12.9 0.7 copy.44.refs_17_
  13.6 0.0 copy-done.1
  13.6 0.7 copy.43.refs_1_
  14.3 91.5 %forward.1 = (bf16[2,512,2048]{2,1,0:T(8,128)(2,1)}, bf16[2,2048,512]{2,1,0:T(8,128)(2,1)}, f32[2,896,512]{2,1,0:T(8,128)}, f32[2,896,512]{2,1,0:T(8,128)}, bf16...) custom-call(bf16[32,49,3072]{2,1,0:T(8,128)(2,1)} %copy.42.refs_0_, ...), custom_call_target="tpu_custom_call" | custom-call | flops 1000000000 | bytes 25000000 | tf_op jit(solution)/shard_map/forward/pallas_call | solution.py:441
  105.8 152.3 %backward.1 = (f32[256,384]{1,0:T(8,128)}, f32[2,64,1024]{2,1,0:T(8,128)}, f32[2,512,128]{2,1,0:T(8,128)}, f32[64,512]{1,0:T(8,128)}, f32[24,512]{1,0:T(8,128)}, /*index=5*/f32[2,256,128]{2,1,0:T(8,128)}) custom-call(bf16[2,512,2048]{2,1,0:T(8,128)(2,1)} %get-tuple-element.37.refs_0_, bf16[2,2048,512]{2,1,0:T(8,128)(2,1)} %get-tuple-element.38.refs_1_, ...), custom_call_target="tpu_custom_call" | custom-call | flops 1000000000 | bytes 50000000 | tf_op jit(solution)/shard_map/backward/pallas_call | solution.py:800
  258.1 2.0 copy.46
  260.1 1.9 copy.45
  262.0 1.5 constant_dynamic-slice_fusion.3
  263.5 0.8 slice.54
  264.3 0.6 constant_dynamic-slice_fusion.2
  264.9 1.5 fusion.1
  266.4 1.4 dynamic-slice_bitcast_fusion.1
  267.7 1.3 constant_dynamic-slice_fusion.1
  269.0 1.5 dynamic-slice_reduce_fusion
  270.5 1.2 slice.45
  271.7 1.9 copy.49
  273.6 1.6 copy.50
  (1 shorter events, 0.0 us)
Async XLA Ops:
  0.7 12.2 %copy-start = (f32[2,49,32]{1,2,0:T(8,128)S(1)}, f32[2,49,32]{1,2,0:T(8,128)}, u32[]{:S(2)}) copy-start(f32[2,49,32]{1,2,0:T(8,128)} %param.25) | copy-start | bytes 37636
  0.7 12.9 %copy-start.1 = (s32[32]{0:T(128)S(1)}, s32[32]{0:T(128)}, u32[]{:S(2)}) copy-start(s32[32]{0:T(128)} %param.20) | copy-start | bytes 388

commit v3 on v2

--- a/solution.py
+++ b/solution.py
@@ -62,14 +62,14 @@
 
 ROW_VEC = dict(b_stem=N0, ln1_g=N1, ln1_b=N3, ln2_g=N5, ln2_b=N7, b_ch2=9, b_ch1=11, lnf_g=19, lnf_b=20, b_head=21, loss=23)
 VEC_ROWS = 24
-TOK = 56
+TOK = 49
 IMAGES = 16
 ROWS = TOK * IMAGES
 BAND = 128
-BANDS = ROWS // BAND
+STRIP = 112
+STRIPS = ROWS // STRIP
 WIDE = 512
 DEEP = 2048
-HALF = ROWS // N2
 GELU_A = 0.7978845608028654
 GELU_B = 0.044715
 
@@ -84,10 +84,41 @@
 
 def gelu_pair(pre):
     square = pre * pre
-    tanh = jnp.tanh(GELU_A * (pre + GELU_B * (square * pre)))
+    tanh = jnp.tanh(pre * (GELU_A + (GELU_A * GELU_B) * square))
     cdf = 0.5 + 0.5 * tanh
-    slope = cdf + (0.5 * pre) * (1.0 - tanh * tanh) * (GELU_A + (3.0 * GELU_A * GELU_B) * square)
-    return pre * cdf, slope
+    value = pre * cdf
+    return value, cdf + value * ((1.0 - tanh) * (GELU_A + (3.0 * GELU_A * GELU_B) * square))
+
+
+def gelu_value(pre):
+    return pre * (0.5 + 0.5 * jnp.tanh(pre * (GELU_A + (GELU_A * GELU_B) * (pre * pre))))
+
+
+def image_rows(b):
+    return pl.ds(b, TOK, stride=IMAGES)
+
+
+def get(ref, rows):
+    return jnp.concatenate([ref[k, rows, :] for k in range(N4)], axis=N1)
+
+
+def put(ref, rows, values):
+    for k in range(N4):
+        ref[k, rows, :] = values[:, k * BAND:(k + N1) * BAND]
+
+
+def strip_rows(i):
+    return pl.ds(aligned(i * STRIP, STRIP), STRIP)
+
+
+def turn(dst, read):
+    whole = ROWS // BAND
+
+    @pl.loop(N0, whole)
+    def _(i):
+        rows = pl.ds(aligned(i * BAND, BAND), BAND)
+        dst[:, rows] = read(rows).astype(F32).T.astype(BF16)
+    dst[:, whole * BAND:] = read(pl.ds(whole * BAND, ROWS % BAND)).astype(F32).T.astype(BF16)
 
 
 def standardize(values):
@@ -111,15 +142,14 @@
 
 
 STEM_W, SMALL, HEAD_W, CHAN1, CHAN2 = N0, N1, N6, (N2, N4), (N3, N5)
-GATHER_SPLITS = (((N0, 128), (128, 128), (256, 128)), ((N0, 72), (72, 64), (136, 64)),
+GATHER_SPLITS = (((N0, 128), (128, 128), (256, 128)), ((N0, 32), (32, 32), (64, 24)),
                  ((N0, 16), (16, 16), (32, 32)), ((N0, 48), (48, 48), (96, 32)),
                  ((N0, 16), (16, 16), (32, 32)), ((N0, 48), (48, 48), (96, 32)), ((N0, 32), (32, 16), (48, 16)))
 GATHERED = len(GATHER_SPLITS)
-PACK_ROWS = 200
-AT_B1, AT_BT, AT_BH, AT_T1, AT_T2 = 16, 18, 20, 24, 136
+PACK_ROWS = 88
+AT_B1, AT_BT, AT_BH, AT_T = 16, 18, 20, 24
 VECTORS = (('b_stem', N1), ('ln1_g', N2), ('ln1_b', N2), ('ln2_g', N2), ('ln2_b', N2), ('b_ch2', N2), ('lnf_g', N1), ('lnf_b', N1))
 CLASSES_HALF = 500
-TOKENS = 49
 TOTAL = 256
 PATCH = 3072
 
@@ -132,21 +162,17 @@
     patch_hbm, labels, f_stem, f1, f2, f_head = grab(N6)
     vec_in = grab(len(VECTORS))
     i_b1, i_bt, i_bh, i_t1, i_t2 = grab(N5)
-    w1_out, w2_out, xa_out, xb_out, patch_out, t1t, t1, t2, bt, vec, gh, hs, d0 = grab(13)
+    w1_out, w2_out, xa_out, xb_out, t1t, t1, t2, bt, vec, gh, hs, d0 = grab(12)
     own_stem, own1, own2, own_head, pack = grab(N5)
     stem_w, small, w1, w2, head_w = grab(N5)
-    pin, padded, pbuf, t2t = grab(N4)
+    pin, t2t = grab(N2)
     xs = grab(N5)
     v, pre, act, pooled = grab(N4)
     send_sem, recv_sem, load_sem, save_sem = grab(N4)
     coords, core = my_position()
     tp = coords[N2]
-    half_images = pin.shape[N0]
-    loads = []
-    for b in range(half_images):
-        copy = pltpu.make_async_copy(patch_hbm.at[tp * half_images + b], pin.at[b], load_sem.at[b])
-        copy.start()
-        loads.append(copy)
+    patch_copy = pltpu.make_async_copy(patch_hbm.at[:, pl.ds(aligned(tp * IMAGES, IMAGES), IMAGES), :], pin, load_sem)
+    patch_copy.start()
 
     own_stem[...] = f_stem[...].astype(BF16)
     own1[...] = f1[...].astype(BF16)
@@ -164,8 +190,9 @@
         width = min(BAND, CLASSES_HALF - k * BAND)
         pack[AT_BH + k:AT_BH + k + N1, :width] = i_bh[:, k * BAND:k * BAND + width]
     for layer in range(N2):
-        pack[AT_T1 + TOK * layer:AT_T1 + TOK * layer + TOKENS, :32] = i_t1[layer]
-        pack[AT_T2 + 32 * layer:AT_T2 + 32 * layer + 32, :TOKENS] = i_t2[layer]
+        at = AT_T + 32 * layer
+        pack[at:at + 32, :TOK] = i_t1[layer]
+        pack[at:at + 32, 64:64 + TOK] = i_t2[layer]
     entry_barrier(coords, core)
 
     own = [own_stem, pack, own1.at[N0], own2.at[N0], own1.at[N1], own2.at[N1], own_head]
@@ -200,9 +227,8 @@
         order = ORDERS[part]
         rank = sum(N2 ** i for i in DIMS if bits[order[i]])
         for step in range(level, N3):
-            move(item, part, bits, level == N0, device_of(shifted(coords, unit(order[step])), core),
-                 N2 ** step - N1 + rank)
-        move(item, part, bits, level == N0, device_of(coords, N1 - core), N7 + rank)
+            move(item, part, bits, False, device_of(shifted(coords, unit(order[step])), core), N2 ** step - N1 + rank)
+        move(item, part, bits, False, device_of(coords, N1 - core), N7 + rank)
 
     def bits_of(part, rank):
         bits = [N0, N0, N0]
@@ -211,8 +237,13 @@
         return tuple(bits)
 
     def send_own(item):
+        none = (N0, N0, N0)
+        for step in DIMS:
+            for part in DIMS:
+                target = device_of(shifted(coords, unit(ORDERS[part][step])), core)
+                move(item, part, none, True, target, N2 ** step - N1)
         for part in DIMS:
-            pass_on(item, part, (N0, N0, N0), N0)
+            move(item, part, none, True, device_of(coords, N1 - core), N7)
 
     def forward(item, level):
         for part in DIMS:
@@ -237,36 +268,19 @@
         copy.start()
         saves.append((src, dst))
 
-    early = (STEM_W, SMALL)
+    early = (SMALL, STEM_W)
     for item in early:
         send_own(item)
-    send_own(CHAN1[N0])
     for item in range(GATHERED):
         place_own(item)
-    padded[...] = jnp.zeros(padded.shape, F32)
-    for item in early:
-        forward(item, N0)
-    send_own(CHAN2[N0])
-
-    def pad_patches(q):
-        for i in range(N2):
-            padded[i * TOK:i * TOK + TOKENS, :] = pin[N2 * q + i].astype(F32)
-        pbuf[pl.ds(aligned(q * N2 * TOK, 16), N2 * TOK), :] = padded[...].astype(BF16)
-    for copy in loads:
-        copy.wait()
-    for item in early:
-        forward(item, N1)
-    send_own(CHAN1[N1])
-    pl.loop(N0, N4)(pad_patches)
+    for level in range(N2):
+        for item in early:
+            forward(item, level)
+    send_own(CHAN1[N0])
     for item in early:
         forward(item, N2)
-    send_own(CHAN2[N1])
-    send_own(HEAD_W)
-    pl.loop(N4, N8)(pad_patches)
-    save(pbuf, patch_out)
-    forward(CHAN1[N0], N0)
-    for item in early:
-        finish(item)
+    send_own(CHAN2[N0])
+    finish(SMALL)
 
     lane32 = lax.broadcasted_iota(jnp.int32, (N1, BAND), N1) // 32
 
@@ -297,81 +311,90 @@
         for layer in range(N2):
             column = AT_BT - AT_B1 + layer
             bt[layer, cols, :] = turned[:, column:column + N1]
-            found = lay_out(q, AT_T1 + TOK * layer, TOK)
-            t1[layer, :, cols] = found.astype(BF16)
-            t1t[layer, cols, :] = found.T.astype(BF16)
-            rows = jnp.concatenate([small[N4 * q + i, AT_T2 + 32 * layer:AT_T2 + 32 * layer + 32, :] for i in range(N4)],
-                                   axis=N0)
-            t2[layer, cols, :] = rows[:, :TOK].astype(BF16)
-            t2t[layer, :, cols] = rows.T[:TOK].astype(BF16)
+            at = AT_T + 32 * layer
+            rows = jnp.concatenate([small[N4 * q + i, at:at + 32, :] for i in range(N4)], axis=N0)
+            back = rows.T
+            t1t[layer, cols, :] = rows[:, :TOK].astype(BF16)
+            t1[layer, :, cols] = back[:TOK].astype(BF16)
+            t2[layer, cols, :] = pltpu.roll(rows, 64, N1)[:, :TOK].astype(BF16)
+            t2t[layer, :, cols] = back[64:64 + TOK].astype(BF16)
 
     def vector(name, at=N0):
         return vec[pl.ds(ROW_VEC[name] + at, N1), :]
 
-    tasks = [lambda: forward(CHAN2[N0], N0), lambda: forward(CHAN1[N0], N1)]
-
-    @pl.loop(N0, N2)
-    def _(h):
-        rows = pl.ds(aligned(h * HALF, HALF), HALF)
-        xs[N0][rows, :] = times(pbuf[rows, :], stem_w[...]) + vector('b_stem')
-        for k, task in enumerate(tasks):
-            pl.when(h == k)(task)
+    forward(CHAN1[N0], N0)
+    finish(STEM_W)
+    patch_copy.wait()
+    cut = TOK // N2 + N1
+    for lo, num, tasks in ((N0, cut, ((CHAN2[N0], N0), (CHAN1[N0], N1))), (cut, TOK - cut, ((CHAN2[N0], N1),))):
+        rows = pl.ds(lo * IMAGES, num * IMAGES)
+        patches = pin[lo:lo + num].reshape(num * IMAGES, PATCH)
+        put(xs[N0], rows, times(patches, stem_w[...]) + vector('b_stem'))
+        for item, level in tasks:
+            forward(item, level)
+        send_own(CHAN2[N1] if lo else CHAN1[N1])
     save(xs[N0], xa_out.at[N0])
 
     def token_mix(layer, tasks):
         source, target = xs[N2 * layer], xs[N2 * layer + N1]
         gain, shift = vector('ln1_g', layer), vector('ln1_b', layer)
 
-        @pl.loop(N0, IMAGES)
-        def _(b):
-            rows = pl.ds(aligned(b * TOK, N8), TOK)
-            here = source[rows, :]
-            norm = (standardize(here)[N0] * gain + shift).astype(BF16)
-            hidden = jax.nn.gelu(times(t1t[layer], norm) + bt[layer]).astype(BF16)
-            target[rows, :] = here + times(t2t[layer], hidden)
-            for k, task in tasks:
-                pl.when(b == k)(task)
+        @pl.loop(N0, IMAGES // N2)
+        def _(pair):
+            rows = [image_rows(N2 * pair + i) for i in range(N2)]
+            here = [get(source, r) for r in rows]
+            norm = [(standardize(x)[N0] * gain + shift).astype(BF16) for x in here]
+            hidden = [gelu_value(times(t1t[layer], n) + bt[layer]).astype(BF16) for n in norm]
+            mixed = [x + times(t2t[layer], h) for x, h in zip(here, hidden)]
+            for r, x in zip(rows, mixed):
+                put(target, r, x)
+            for k, task in enumerate(tasks):
+                pl.when(pair == k)(task)
 
     def channel_mix(layer, tasks):
         source, target = xs[N2 * layer + N1], xs[N2 * layer + N2]
         gain, shift = vector('ln2_g', layer), vector('ln2_b', layer)
 
-        @pl.loop(N0, BANDS)
+        @pl.loop(N0, STRIPS)
         def _(i):
-            rows = pl.ds(aligned(i * BAND, BAND), BAND)
-            here = source[rows, :]
+            rows = strip_rows(i)
+            here = get(source, rows)
             v[rows, :] = (standardize(here)[N0] * gain + shift).astype(BF16)
-            target[rows, :] = here + vector('b_ch2', layer)
+            put(target, rows, here + vector('b_ch2', layer))
 
         @pl.loop(N0, N4)
         def _(j):
             cols = pl.ds(aligned(j * WIDE, WIDE), WIDE)
             bias = vector('b_ch1', N4 * layer + j)
-            for half in range(N2):
-                rows = pl.ds(half * HALF, HALF)
-                pre[...] = times(v[rows, :], w1[layer, :, cols])
-
-                @pl.loop(N0, HALF // 32)
-                def _(i):
-                    part = pl.ds(aligned(i * 32, 32), 32)
-                    act[part, :] = jax.nn.gelu(pre[part, :] + bias).astype(BF16)
-                target[rows, :] = target[rows, :] + times(act[...], w2[layer, cols, :])
-            for k, task in tasks:
+            pre[...] = times(v[...], w1[layer, :, cols])
+
+            @pl.loop(N0, STRIPS)
+            def _(i):
+                rows = strip_rows(i)
+                act[rows, :] = gelu_value(pre[rows, :] + bias).astype(BF16)
+            everything = pl.ds(N0, ROWS)
+            put(target, everything, get(target, everything) + times(act[...], w2[layer, cols, :]))
+            for k, task in enumerate(tasks):
                 pl.when(j == k)(task)
 
-    token_mix(N0, [(N1, lambda: forward(CHAN2[N0], N1)), (N4, lambda: forward(CHAN1[N0], N2)),
-                  (N6, lambda: forward(CHAN2[N0], N2)), (N8, lambda: forward(CHAN1[N1], N0)),
-                  (10, lambda: forward(CHAN2[N1], N0)), (12, lambda: forward(HEAD_W, N0)),
-                  (14, lambda: forward(CHAN1[N1], N1))])
+    def both(first, second):
+        def run():
+            first()
+            second()
+        return run
+
+    def step(item, level):
+        return lambda: forward(item, level)
+    token_mix(N0, [step(CHAN1[N0], N2), step(CHAN2[N0], N2), both(step(CHAN1[N1], N0), lambda: send_own(HEAD_W)),
+                  step(CHAN2[N1], N0), step(CHAN1[N1], N1), step(CHAN2[N1], N1), step(HEAD_W, N0), step(CHAN1[N1], N2)])
     save(xs[N1], xb_out.at[N0])
     finish(CHAN1[N0])
     finish(CHAN2[N0])
     save(w1.at[N0], w1_out.at[N0])
     save(w2.at[N0], w2_out.at[N0])
-    channel_mix(N0, [(N0, lambda: forward(CHAN2[N1], N1)), (N1, lambda: forward(HEAD_W, N1)),
-                    (N2, lambda: forward(CHAN1[N1], N2)), (N3, lambda: forward(CHAN2[N1], N2))])
+    channel_mix(N0, [step(CHAN2[N1], N2), step(HEAD_W, N1), step(HEAD_W, N2)])
     save(xs[N2], xa_out.at[N1])
-    token_mix(N1, [(N0, lambda: forward(HEAD_W, N2))])
+    token_mix(N1, [])
     save(xs[N3], xb_out.at[N1])
     for item in (CHAN1[N1], CHAN2[N1], HEAD_W):
         finish(item)
@@ -379,14 +402,13 @@
     save(w2.at[N1], w2_out.at[N1])
     channel_mix(N1, [])
 
-    real_row = lax.broadcasted_iota(jnp.int32, (TOK, N1), N0) < TOKENS
-
-    @pl.loop(N0, IMAGES)
-    def _(b):
-        here = xs[N4][pl.ds(aligned(b * TOK, N8), TOK), :]
-        pooled[pl.ds(b, N1), :] = row_sum(jnp.where(real_row, here, 0.0)) * (1.0 / TOKENS)
+    pooled[...] = jnp.zeros(pooled.shape, F32)
+
+    @pl.loop(N0, TOK)
+    def _(t):
+        pooled[...] = pooled[...] + get(xs[N4], pl.ds(aligned(t * IMAGES, IMAGES), IMAGES))
     gain = vector('lnf_g')
-    standard, inv_std = standardize(pooled[...])
+    standard, inv_std = standardize(pooled[...] * (1.0 / TOK))
     norm = standard * gain + vector('lnf_b')
     norm_bf = norm.astype(BF16)
     lane = lax.broadcasted_iota(jnp.int32, (IMAGES, WIDE), N1)
@@ -414,7 +436,7 @@
     hs[lnf + N1:lnf + N2, :] = row_sum(back)
     at = ROW_VEC['loss']
     hs[at:at + N1, :] = jnp.broadcast_to(row_sum(losses) * (1.0 / TOTAL), (N1, WIDE))
-    d0[...] = norm_back(back, gain, standard, inv_std) * (1.0 / TOKENS)
+    d0[...] = norm_back(back, gain, standard, inv_std) * (1.0 / TOK)
 
     for k, (src, dst) in enumerate(saves):
         pltpu.make_async_copy(src, dst, save_sem.at[k]).wait()
@@ -431,26 +453,26 @@
 def forward_all(*operands):
     any_spec, vmem = pl.BlockSpec(memory_space=pl.ANY), pl.BlockSpec(memory_space=pltpu.VMEM)
     shape = jax.ShapeDtypeStruct
-    plane = (ROWS, WIDE)
-    outs = [shape((N2, WIDE, DEEP), BF16), shape((N2, DEEP, WIDE), BF16), shape((N2,) + plane, F32),
-            shape((N2,) + plane, F32), shape((ROWS, PATCH), BF16), shape((N2, 256, TOK), BF16),
+    plane, blocks = (ROWS, WIDE), (N4, ROWS, BAND)
+    outs = [shape((N2, WIDE, DEEP), BF16), shape((N2, DEEP, WIDE), BF16), shape((N2,) + blocks, F32),
+            shape((N2,) + blocks, F32), shape((N2, 256, TOK), BF16),
             shape((N2, TOK, 256), BF16), shape((N2, 256, TOK), BF16), shape((N2, 256, N1), F32),
             shape((VEC_ROWS, WIDE), F32), shape((WIDE, N2 * WIDE), F32), shape((VEC_ROWS, WIDE), F32),
             shape((IMAGES, WIDE), F32)]
     dma = pltpu.SemaphoreType.DMA
     return pl.pallas_call(
         forward_kernel, out_shape=outs, in_specs=[any_spec] + [vmem] * (len(operands) - N1),
-        out_specs=[any_spec] * N5 + [vmem] * N8,
+        out_specs=[any_spec] * N4 + [vmem] * N8,
         scratch_shapes=[
             pltpu.VMEM((384, 256), BF16), pltpu.VMEM((N2, 64, 1024), BF16), pltpu.VMEM((N2, 128, WIDE), BF16),
             pltpu.VMEM((64, WIDE), BF16), pltpu.VMEM((PACK_ROWS, BAND), F32),
             pltpu.VMEM((PATCH, WIDE), BF16), pltpu.VMEM((16, PACK_ROWS, BAND), F32), pltpu.VMEM((N2, WIDE, DEEP), BF16),
             pltpu.VMEM((N2, DEEP, WIDE), BF16), pltpu.VMEM((WIDE, N2 * WIDE), BF16),
-            pltpu.VMEM((IMAGES, TOKENS, PATCH), BF16), pltpu.VMEM((N2 * TOK, PATCH), F32), pltpu.VMEM((ROWS, PATCH), BF16),
-            pltpu.VMEM((N2, TOK, 256), BF16)] + [pltpu.VMEM(plane, F32)] * N5 + [
-            pltpu.VMEM(plane, BF16), pltpu.VMEM((HALF, WIDE), F32), pltpu.VMEM((HALF, WIDE), BF16),
+            pltpu.VMEM((TOK, IMAGES, PATCH), BF16),
+            pltpu.VMEM((N2, TOK, 256), BF16)] + [pltpu.VMEM(blocks, F32)] * N5 + [
+            pltpu.VMEM(plane, BF16), pltpu.VMEM(plane, F32), pltpu.VMEM(plane, BF16),
             pltpu.VMEM((IMAGES, WIDE), F32),
-            dma, dma((GATHERED, N3, 15)), dma((IMAGES,)), dma((9,))],
+            dma, dma((GATHERED, N3, 15)), dma, dma((N8,))],
         compiler_params=pltpu.CompilerParams(collective_id=N0, has_side_effects=True, vmem_limit_bytes=67043328),
         cost_estimate=pl.CostEstimate(flops=10 ** 9, bytes_accessed=25 * 10 ** N6, transcendentals=N0),
         name='forward')(*operands)
@@ -472,7 +494,7 @@
     o_stem, o1, o2, oh, osum, otok = grab(N6)
     mine, peer = grab(ITEMS), grab(ITEMS)
     boxes = [[grab(N3) for _ in DIMS] for _ in range(ITEMS)]
-    w1, w2, xa, xb, grad, acc, v, vt, dout, dout_t, pre, dact, act, dpre, g1, g2, pbuf, gs = grab(18)
+    w1, w2, xa, xb, grad, acc, v, vt, dout, dout_t, pre, dact, act, dpre, g1, g2, pbuf = grab(17)
     tacc1, tacc2, bacc, sbox, tbox = grab(N5)
     send_sem, hop_sem, peer_sem, pair_sem, load_sem, red_send, red_recv = grab(N7)
     coords, core = my_position()
@@ -579,11 +601,10 @@
                 heads.append(load(head_view(y * N4 + x * N2 + core).at[:, pl.ds(z * WIDE, WIDE)],
                                   mine[HEAD].at[z, y, x], N5 + slot))
     osum[...] = hs[...]
-    real_row = lax.broadcasted_iota(jnp.int32, (TOK, N1), N0) < TOKENS
-
-    @pl.loop(N0, IMAGES)
-    def _(b):
-        grad[pl.ds(aligned(b * TOK, N8), TOK), :] = jnp.where(real_row, d0[pl.ds(b, N1), :], 0.0)
+
+    @pl.loop(N0, TOK)
+    def _(t):
+        put(grad, pl.ds(aligned(t * IMAGES, IMAGES), IMAGES), d0[...])
 
     def head_start():
         for y in range(N2):
@@ -610,39 +631,35 @@
     def channel_back(layer, steps):
         gain, shift = vec[pl.ds(ROW_VEC['ln2_g'] + layer, N1), :], vec[pl.ds(ROW_VEC['ln2_b'] + layer, N1), :]
 
-        @pl.loop(N0, BANDS)
+        @pl.loop(N0, STRIPS)
         def _(i):
-            rows = pl.ds(aligned(i * BAND, BAND), BAND)
-            standard, _ = standardize(xb[rows, :])
-            norm = standard * gain + shift
-            v[rows, :] = norm.astype(BF16)
-            vt[:, rows] = norm.T.astype(BF16)
-            here = grad[rows, :]
+            rows = strip_rows(i)
+            standard, _ = standardize(get(xb, rows))
+            v[rows, :] = (standard * gain + shift).astype(BF16)
+            here = get(grad, rows)
             dout[rows, :] = here.astype(BF16)
-            dout_t[:, rows] = here.T.astype(BF16)
             add_row('b_ch2', layer, row_sum(here))
-            acc[rows, :] = jnp.zeros((BAND, WIDE), F32)
+            acc[rows, :] = jnp.zeros((STRIP, WIDE), F32)
+        turn(vt, lambda rows: v[rows, :])
+        turn(dout_t, lambda rows: dout[rows, :])
 
         @pl.loop(N0, N4)
         def _(j):
             cols = pl.ds(aligned(j * WIDE, WIDE), WIDE)
             bias = vec[pl.ds(ROW_VEC['b_ch1'] + N4 * layer + j, N1), :]
             bacc[...] = jnp.zeros(bacc.shape, F32)
-            for half in range(N2):
-                rows = pl.ds(half * HALF, HALF)
-                pre[...] = times(v[rows, :], w1[:, cols])
-                dact[...] = by_rows(dout[rows, :], w2[cols, :])
-
-                @pl.loop(N0, HALF // 32)
-                def _(i):
-                    small = pl.ds(aligned(i * 32, 32), 32)
-                    value, slope = gelu_pair(pre[small, :] + bias)
-                    change = dact[small, :] * slope
-                    where = pl.ds(aligned(half * HALF + i * 32, 32), 32)
-                    act[where, :] = value.astype(BF16)
-                    dpre[where, :] = change.astype(BF16)
-                    bacc[...] = bacc[...] + jnp.sum(change.reshape(N4, N8, WIDE), axis=N0)
-                acc[rows, :] = acc[rows, :] + by_rows(dpre[rows, :], w1[:, cols])
+            pre[...] = times(v[...], w1[:, cols])
+            dact[...] = by_rows(dout[...], w2[cols, :])
+
+            @pl.loop(N0, STRIPS)
+            def _(i):
+                rows = strip_rows(i)
+                value, slope = gelu_pair(pre[rows, :] + bias)
+                change = dact[rows, :] * slope
+                act[rows, :] = value.astype(BF16)
+                dpre[rows, :] = change.astype(BF16)
+                bacc[...] = bacc[...] + jnp.sum(change.reshape(STRIP // N8, N8, WIDE), axis=N0)
+            acc[...] = acc[...] + by_rows(dpre[...], w1[:, cols])
             add_row('b_ch1', N4 * layer + j, row_sum(bacc[...]))
 
             @pl.when(j > N0)
@@ -668,43 +685,43 @@
             add_peer(item)
             phase_send(item, N0)
 
-        @pl.loop(N0, BANDS)
+        @pl.loop(N0, STRIPS)
         def _(i):
-            rows = pl.ds(aligned(i * BAND, BAND), BAND)
-            standard, inv_std = standardize(xb[rows, :])
+            rows = strip_rows(i)
+            standard, inv_std = standardize(get(xb, rows))
             here = acc[rows, :]
             add_row('ln2_g', layer, row_sum(here * standard))
             add_row('ln2_b', layer, row_sum(here))
-            grad[rows, :] = grad[rows, :] + norm_back(here, gain, standard, inv_std)
+            put(grad, rows, get(grad, rows) + norm_back(here, gain, standard, inv_std))
 
     def token_back(layer, steps):
         gain, shift = vec[pl.ds(ROW_VEC['ln1_g'] + layer, N1), :], vec[pl.ds(ROW_VEC['ln1_b'] + layer, N1), :]
         tacc1[...] = jnp.zeros(tacc1.shape, F32)
         tacc2[...] = jnp.zeros(tacc2.shape, F32)
-        pre256, change256 = pre.at[pl.ds(N0, 256), :], dact.at[pl.ds(N0, 256), :]
-
-        @pl.loop(N0, IMAGES)
-        def _(b):
-            rows = pl.ds(aligned(b * TOK, N8), TOK)
-            standard, inv_std = standardize(xa[rows, :])
-            norm = (standard * gain + shift).astype(BF16)
-            here = grad[rows, :]
-            here_bf = here.astype(BF16)
-            value, slope = gelu_pair(times(t1t[layer], norm) + bt[layer])
-            change = times(t2[layer], here_bf) * slope
-            change_bf = change.astype(BF16)
-            total = change[:, :BAND]
-            for k in range(N1, N4):
-                total = total + change[:, k * BAND:(k + N1) * BAND]
+
+        @pl.loop(N0, IMAGES // N2)
+        def _(pair):
+            rows = [image_rows(N2 * pair + i) for i in range(N2)]
+            both = range(len(rows))
+            inputs, heres = [get(xa, r) for r in rows], [get(grad, r) for r in rows]
+            standards, invs = zip(*[standardize(x) for x in inputs])
+            norms = [(x * gain + shift).astype(BF16) for x in standards]
+            heres_bf = [x.astype(BF16) for x in heres]
+            values, slopes = zip(*[gelu_pair(times(t1t[layer], x) + bt[layer]) for x in norms])
+            changes = [times(t2[layer], x) * slope for x, slope in zip(heres_bf, slopes)]
+            changes_bf = [x.astype(BF16) for x in changes]
+            total = sum(x[:, k * BAND:(k + N1) * BAND] for x in changes for k in range(N4))
+            d_norms = [times(t1[layer], x) for x in changes_bf]
             tacc1[:, BAND:] = tacc1[:, BAND:] + total
-            tacc1[:, :TOK] = tacc1[:, :TOK] + by_rows(change_bf, norm)
-            tacc2[:, :TOK] = tacc2[:, :TOK] + by_rows(value.astype(BF16), here_bf)
-            d_norm = times(t1[layer], change_bf)
-            add_row('ln1_g', layer, row_sum(d_norm * standard))
-            add_row('ln1_b', layer, row_sum(d_norm))
-            grad[rows, :] = here + norm_back(d_norm, gain, standard, inv_std)
+            tacc1[:, :TOK] = tacc1[:, :TOK] + sum(by_rows(changes_bf[i], norms[i]) for i in both)
+            tacc2[:, :TOK] = tacc2[:, :TOK] + sum(by_rows(values[i].astype(BF16), heres_bf[i]) for i in both)
+            add_row('ln1_g', layer, sum(row_sum(d_norms[i] * standards[i]) for i in both))
+            add_row('ln1_b', layer, sum(row_sum(d_norms[i]) for i in both))
+            results = [heres[i] + norm_back(d_norms[i], gain, standards[i], invs[i]) for i in both]
+            for r, x in zip(rows, results):
+                put(grad, r, x)
             for k, step in steps:
-                pl.when(b == k)(step)
+                pl.when(pair == k)(step)
         lane = lax.broadcasted_iota(jnp.int32, (256, BAND), N1)
         bias_grad = jnp.sum(tacc1[:, BAND:], axis=N1, keepdims=True)
         otok[layer] = (jnp.where(lane < TOK, tacc1[:, :BAND], 0.0)
@@ -721,7 +738,7 @@
                      lambda: advance([HEAD], N2, [oh])])
     again = [load(w1_hbm.at[N0], w1, N0), load(w2_hbm.at[N0], w2, N1), load(xb_hbm.at[N0], xb, N2)]
     xa_copy.wait()
-    token_back(N1, [(11, lambda: advance(layer1, N0))])
+    token_back(N1, [(N5, lambda: advance(layer1, N0))])
     reduce_send(late, N0)
     xa_copy = load(xa_hbm.at[N0], xa, N4)
     for copy in again:
@@ -736,40 +753,48 @@
         reduce_step(late, N2)
     channel_back(N0, [lambda: reduce_step(late, N0), second, third, lambda: reduce_step(late, N3)])
     xa_copy.wait()
-    token_back(N0, [(11, lambda: advance(layer0, N0))])
-
-    @pl.loop(N0, BANDS)
+    token_back(N0, [(N5, lambda: advance(layer0, N0))])
+
+    @pl.loop(N0, STRIPS)
     def _(i):
-        rows = pl.ds(aligned(i * BAND, BAND), BAND)
-        here = grad[rows, :]
-        dout_t[:, rows] = here.T.astype(BF16)
-        add_row('b_stem', N0, row_sum(here))
+        add_row('b_stem', N0, row_sum(get(grad, strip_rows(i))))
+    turn(dout_t, lambda rows: get(grad, rows))
     reduce_send(final, N0)
 
     def patch_load(k):
         f = (k % N4) * N2 + (other if k < N4 else core)
-        return load(patch_hbm.at[:, pl.ds(aligned(f * 384, BAND), 384)], pbuf.at[k % N2], k % N2)
+        images = pl.ds(aligned(coords[N2] * IMAGES, IMAGES), IMAGES)
+        return load(patch_hbm.at[:, images, pl.ds(aligned(f * 384, BAND), 384)], pbuf.at[k % N2], k % N2)
+    def stem_part(z):
+        return g2.at[pl.ds(z * 256, 256), pl.ds(N0, 384)]
+
+    def stem_left():
+        for z in range(N2):
+            left(stem_part(z), pair_sem.at[N8])
     copies = {N0: patch_load(N0)}
     for k in range(N8):
         if k < N7:
             copies[k + N1] = patch_load(k + N1)
         copies[k].wait()
         y, x = (k % N4) // N2, k % N2
-        result = times(dout_t[...], pbuf[k % N2]).reshape(N2, 256, 384)
+        result = times(dout_t[...], pbuf[k % N2].reshape(ROWS, 384))
         if k < N4:
             if k > N0:
-                left(gs, pair_sem.at[N8])
-            gs[...] = result
-            start(gs, peer[STEM].at[:, y, x], pair_sem.at[k], partner, pair_sem.at[N8])
+                stem_left()
+            g2[:, :384] = result
+            for z in range(N2):
+                start(stem_part(z), peer[STEM].at[z, y, x], pair_sem.at[N2 * k + z], partner, pair_sem.at[N8])
         else:
-            mine[STEM][:, y, x] = result
+            for z in range(N2):
+                mine[STEM][z, y, x] = result[z * 256:z * 256 + 256]
         if k == N3:
-            left(gs, pair_sem.at[N8])
+            stem_left()
             reduce_step(final, N0)
         if k == N5:
             advance(layer0, N1)
     for k in range(N4):
-        arrived(peer[STEM].at[:, k // N2, k % N2], pair_sem.at[k])
+        for z in range(N2):
+            arrived(peer[STEM].at[z, k // N2, k % N2], pair_sem.at[N2 * k + z])
     add_peer(STEM)
     phase_send(STEM, N0)
     reduce_step(final, N1)
@@ -792,19 +817,18 @@
     boxes = [pltpu.VMEM((N2,) * (N2 - phase) + (ITEM_SPLITS[item][part][N1], ITEM_SHAPES[item][N1]), F32)
              for item in range(ITEMS) for part in DIMS for phase in DIMS]
     slots = [pltpu.VMEM((N2, N2, N2) + shape, F32) for shape in ITEM_SHAPES]
-    plane = pltpu.VMEM((ROWS, WIDE), F32)
+    plane, blocks = pltpu.VMEM((ROWS, WIDE), F32), pltpu.VMEM((N4, ROWS, BAND), F32)
     plane_bf, turned_bf = pltpu.VMEM((ROWS, WIDE), BF16), pltpu.VMEM((WIDE, ROWS), BF16)
-    half = pltpu.VMEM((HALF, WIDE), F32)
     dma = pltpu.SemaphoreType.DMA
     outs = ((256, 384), (N2, 64, 1024), (N2, 512, 128), (64, 512), (VEC_ROWS, WIDE), (N2, 256, 128))
     return pl.pallas_call(
         backward_kernel, out_shape=[jax.ShapeDtypeStruct(s, F32) for s in outs],
         in_specs=[any_spec] * N2 + [vmem] * N5 + [any_spec] * N2 + [vmem] + [any_spec] * N2 + [vmem], out_specs=[vmem] * len(outs),
         scratch_shapes=slots + slots + boxes + [
-            pltpu.VMEM((WIDE, DEEP), BF16), pltpu.VMEM((DEEP, WIDE), BF16), plane, plane, plane, plane,
-            plane_bf, turned_bf, plane_bf, turned_bf, half, half, plane_bf, plane_bf,
+            pltpu.VMEM((WIDE, DEEP), BF16), pltpu.VMEM((DEEP, WIDE), BF16), blocks, blocks, blocks, plane,
+            plane_bf, turned_bf, plane_bf, turned_bf, plane, plane, plane_bf, plane_bf,
             pltpu.VMEM((N2, N2, N2, 64, WIDE), F32), pltpu.VMEM((WIDE, WIDE), F32),
-            pltpu.VMEM((N2, ROWS, 384), BF16), pltpu.VMEM((N2, 256, 384), F32),
+            pltpu.VMEM((N2, TOK, IMAGES, 384), BF16),
             pltpu.VMEM((256, 256), F32), pltpu.VMEM((256, 128), F32), pltpu.VMEM((N8, WIDE), F32),
             pltpu.VMEM((N4, VEC_ROWS, WIDE), F32), pltpu.VMEM((N2, N4, 256, 128), F32),
             dma, dma((ITEMS, N3, N3)), dma((N2, N3, N4)), dma((9,)), dma((13,)), dma((N3,)), dma((N3, N4))],
@@ -813,6 +837,49 @@
         name='backward')(*operands)
 
 
+def finish_kernel(*refs):
+    take = iter(refs)
+
+    def grab(count):
+        return [next(take) for _ in range(count)]
+    s_stem, s1, s2, sh, osum, otok = grab(N6)
+    loss, o_stem, o1, o2, oh = grab(N5)
+    vec_out = grab(len(VECTORS))
+    o_b1, o_bt, o_bh, o_t1, o_t2 = grab(N5)
+    tp, fsdp = lax.axis_index('tp'), lax.axis_index('fsdp')
+    owner = tp * N8 + fsdp
+    o_stem[...] = s_stem[...].T
+    o1[...] = s1[...]
+    oh[...] = sh[:, :CLASSES_HALF]
+    block = pltpu.roll(osum[:, pl.ds(aligned(owner // N4 * BAND, BAND), BAND)], BAND - 32 * lax.rem(owner, N4), N1)
+    for ref, (name, num) in zip(vec_out, VECTORS):
+        at = ROW_VEC[name]
+        ref[...] = block[at:at + num, :32]
+    deep = osum[:, pl.ds(aligned(lax.rem(owner, N4) * BAND, BAND), BAND)]
+    index = lax.broadcasted_iota(jnp.int32, (VEC_ROWS, N1), N0)
+    head_row = osum[pl.ds(ROW_VEC['b_head'] + tp, N1), :]
+    o_bh[...] = head_row[:, :CLASSES_HALF]
+    at = ROW_VEC['loss']
+    loss[...] = osum[at:at + N1, :N1]
+    for layer in range(N2):
+        o2[layer] = s2[layer].T
+        chosen = index == ROW_VEC['b_ch1'] + N4 * layer + owner // N4
+        o_b1[layer:layer + N1, :] = row_sum(jnp.where(chosen, deep, 0.0))
+        found = otok[layer, pl.ds(aligned(fsdp * 32, 32), 32), :]
+        o_t1[layer] = found[:, :TOK]
+        o_t2[layer] = pltpu.roll(found, 64, N1)[:, :TOK]
+        o_bt[layer:layer + N1, :] = found.T[BAND - N8:BAND - N7, :]
+
+
+def finish_all(*operands):
+    vmem = pl.BlockSpec(memory_space=pltpu.VMEM)
+    shapes = [(N1, N1), (384, 256), (N2, 64, 1024), (N2, BAND, WIDE), (64, CLASSES_HALF)]
+    shapes += [(num, 32) for _, num in VECTORS]
+    shapes += [(N2, BAND), (N2, 32), (N1, CLASSES_HALF), (N2, 32, TOK), (N2, 32, TOK)]
+    return pl.pallas_call(finish_kernel, out_shape=[jax.ShapeDtypeStruct(shape, F32) for shape in shapes],
+                          in_specs=[vmem] * len(operands), out_specs=[vmem] * len(shapes), name='finish')(*operands)
+
+
 def weight_specs():
     vec_spec = P(CHANNEL_AXES)
     layer_vec = P(None, CHANNEL_AXES)
@@ -826,26 +893,16 @@
              ln2_g, ln2_b, w_ch1, b_ch1, w_ch2, b_ch2, lnf_g, lnf_b, w_head, b_head):
         def flat(values):
             return values.reshape(N1, -N1)
-        tp, fsdp = lax.axis_index('tp'), lax.axis_index('fsdp')
-        w1, w2, xa, xb, padded, t1t, t1, t2, bt, vec, gh, hs, d0 = forward_all(
-            patches, labels.reshape(-N1, N1), w_stem, w_ch1, w_ch2, w_head, flat(b_stem), ln1_g, ln1_b, ln2_g, ln2_b,
-            b_ch2, flat(lnf_g), flat(lnf_b), b_ch1, b_tok1, flat(b_head), w_tok1, w_tok2)
-        o_stem, o1, o2, oh, osum, otok = backward_all(w1, w2, t1t, t1, t2, bt, vec, xa, xb, d0, padded, gh, hs)
-        tokens = TOKENS
-        owner = tp * N8 + fsdp
-        lanes = lax.dynamic_slice_in_dim(osum, owner * 32, 32, N1)
-        found = {name: lanes[ROW_VEC[name]:ROW_VEC[name] + num].reshape((num, 32) if num == N2 else (32,))
-                 for name, num in VECTORS}
-        deep = osum[ROW_VEC['b_ch1']:ROW_VEC['lnf_g']].reshape(N2, DEEP)
-        found['b_ch1'] = lax.dynamic_slice_in_dim(deep, owner * 128, 128, N1)
-        found['b_head'] = lax.dynamic_slice_in_dim(osum, ROW_VEC['b_head'] + tp, N1, N0)[N0, :500]
-        tok_rows = lax.dynamic_slice_in_dim(otok, fsdp * 32, 32, N1)
-        found['w_tok1'] = tok_rows[:, :, :tokens].swapaxes(N1, N2)
-        found['w_tok2'] = tok_rows[:, :, 64:64 + tokens]
-        found['b_tok1'] = tok_rows[:, :, BAND - N8]
-        found['w_ch1'], found['w_ch2'] = o1, o2.swapaxes(N1, N2)
-        return tuple([osum[ROW_VEC['loss'], N0], o_stem.T, found['b_stem']] + [found[name] for name in LAYER_NAMES]
-                     + [found['lnf_g'], found['lnf_b'], oh[:, :500], found['b_head']])
+        by_token = patches.swapaxes(N0, N1)
+        w1, w2, xa, xb, t1t, t1, t2, bt, vec, gh, hs, d0 = forward_all(
+            by_token, labels.reshape(-N1, N1), w_stem, w_ch1, w_ch2, w_head, flat(b_stem), ln1_g, ln1_b, ln2_g, ln2_b,
+            b_ch2, flat(lnf_g), flat(lnf_b), b_ch1, b_tok1, flat(b_head), w_tok1.swapaxes(N1, N2), w_tok2)
+        sums = backward_all(w1, w2, t1t, t1, t2, bt, vec, xa, xb, d0, by_token, gh, hs)
+        (loss, g_stem, g_ch1, g_ch2, g_head, gb_stem, g1_g, g1_b, g2_g, g2_b, gb_ch2, gf_g, gf_b,
+         gb_ch1, gb_tok1, gb_head, g_tok1, g_tok2) = finish_all(*sums)
+        return (loss.reshape(()), g_stem, gb_stem.reshape(-N1), g1_g, g1_b, g_tok1.swapaxes(N1, N2), gb_tok1, g_tok2,
+                g2_g, g2_b, g_ch1, gb_ch1, g_ch2, gb_ch2, gf_g.reshape(-N1), gf_b.reshape(-N1), g_head,
+                gb_head.reshape(-N1))
 
     specs = weight_specs()
     return jax.shard_map(step, mesh=mesh, in_specs=(P('fsdp', None, None), P('fsdp')) + specs,

time: 276 us -> 234 us (0.85)
  local copies, waits for them, and re-layouts: 30.7 us -> 1.34 us
  Pallas kernels: 244 us -> 231 us
    unnamed x10 -> x0, local copies, waits for them, and re-layouts: 20.3 us -> none
    pallas_call x1, Pallas kernels: 91.5 us -> 80.8 us  [forward_all(): pl.pallas_call(forward_kernel, out_shape=outs, in_specs=[any_spec] + [vme...]
    slice x6 -> x0, local copies, waits for them, and re-layouts: 7.74 us -> none  [the longest x1 1.53 us: step(): found['w_tok2'] = tok_rows[:, :, 64:64 + tokens]]
    pallas_call x1, Pallas kernels: 152 us -> 147 us  [backward_all(): pl.pallas_call(backward_kernel, out_shape=[jax.ShapeDtypeStruct(s, F32) f...]
    pallas_call x0 -> x1, Pallas kernels: none -> 2.87 us  [finish_all(): pl.pallas_call(finish_kernel, out_shape=[jax.ShapeDtypeStruct(shape, F32)...]
where the time goes in v3:
time: 234 us; the launch traced here: 233 us
  Pallas kernels  231 us (99%)
    pallas_call x1, Pallas kernels, backward_all(): pl.pallas_call(backward_kernel, out_shape=[jax.ShapeDtypeStruct(s, F32) f...  147 us
    pallas_call x1, Pallas kernels, forward_all(): pl.pallas_call(forward_kernel, out_shape=outs, in_specs=[any_spec] + [vme...  80.8 us

profile of v3, /device:TPU:0, one launch (start us, length us, event | category | flops | bytes accessed | tf_op | source)
XLA Modules:
  0.0 233.3 jit_solution(16289952288167470751)
XLA Ops:
  0.7 1.3 copy.37.refs_1_
  2.0 80.8 %forward.1 = (bf16[2,512,2048]{2,1,0:T(8,128)(2,1)}, bf16[2,2048,512]{2,1,0:T(8,128)(2,1)}, f32[2,4,784,128]{3,2,1,0:T(8,128)}, f32[2,4,784,128]{3,2,1,0:T(8,128...) custom-call(bf16[49,32,3072]{2,1,0:T(8,128)(2,1)} %bitcast.13, ...), custom_call_target="tpu_custom_call" | custom-call | flops 1000000000 | bytes 25000000 | tf_op jit(solution)/shard_map/forward/pallas_call | solution.py:463
  82.8 147.5 %backward.1 = (f32[256,384]{1,0:T(8,128)}, f32[2,64,1024]{2,1,0:T(8,128)}, f32[2,512,128]{2,1,0:T(8,128)}, f32[64,512]{1,0:T(8,128)}, f32[24,512]{1,0:T(8,128)}, /*index=5*/f32[2,256,128]{2,1,0:T(8,128)}) custom-call(bf16[2,512,2048]{2,1,0:T(8,128)(2,1)} %get-tuple-element.54.refs_0_, bf16[2,2048,512]{2,1,0:T(8,128)(2,1)} %get-tuple-element.55.refs_1_, ...), custom_call_target="tpu_custom_call" | custom-call | flops 1000000000 | bytes 50000000 | tf_op jit(solution)/shard_map/backward/pallas_call | solution.py:824
  230.3 2.9 %finish.1 = (f32[1,1]{1,0:T(1,128)}, f32[384,256]{1,0:T(8,128)}, f32[2,64,1024]{2,1,0:T(8,128)}, f32[2,128,512]{2,1,0:T(8,128)}, f32[64,500]{1,0:T(8,128)}, /*in...) custom-call(f32[256,384]{1,0:T(8,128)} %get-tuple-element.66.refs_0_, ...), custom_call_target="tpu_custom_call" | custom-call | tf_op jit(solution)/shard_map/finish/pallas_call | solution.py:879

commit v4 on v3

--- a/solution.py
+++ b/solution.py
@@ -52,12 +52,15 @@
     return tuple((i + j) % N2 for i, j in zip(a, b))
 
 
-def entry_barrier(coords, core):
+def barrier_signal(coords, core):
     barrier = pltpu.get_barrier_semaphore()
     for dim in range(N3):
         pl.semaphore_signal(barrier, inc=N1, device_id=device_of(shifted(coords, unit(dim)), core), device_id_type=MESH)
     pl.semaphore_signal(barrier, inc=N1, device_id=device_of(coords, N1 - core), device_id_type=MESH)
-    pl.semaphore_wait(barrier, N4)
+
+
+def barrier_wait():
+    pl.semaphore_wait(pltpu.get_barrier_semaphore(), N4)
 
 
 ROW_VEC = dict(b_stem=N0, ln1_g=N1, ln1_b=N3, ln2_g=N5, ln2_b=N7, b_ch2=9, b_ch1=11, lnf_g=19, lnf_b=20, b_head=21, loss=23)
@@ -171,6 +174,7 @@
     send_sem, recv_sem, load_sem, save_sem = grab(N4)
     coords, core = my_position()
     tp = coords[N2]
+    barrier_signal(coords, core)
     patch_copy = pltpu.make_async_copy(patch_hbm.at[:, pl.ds(aligned(tp * IMAGES, IMAGES), IMAGES), :], pin, load_sem)
     patch_copy.start()
 
@@ -193,7 +197,7 @@
         at = AT_T + 32 * layer
         pack[at:at + 32, :TOK] = i_t1[layer]
         pack[at:at + 32, 64:64 + TOK] = i_t2[layer]
-    entry_barrier(coords, core)
+    barrier_wait()
 
     own = [own_stem, pack, own1.at[N0], own2.at[N0], own1.at[N1], own2.at[N1], own_head]
 
@@ -208,27 +212,34 @@
             return w2.at[CHAN2.index(item), pl.ds(aligned((tp * N8 + fsdp) * 128 + lo, 16), num), :]
         return head_w.at[pl.ds(aligned(fsdp * 64 + lo, 16), num), pl.ds(aligned(tp * WIDE, 128), WIDE)]
 
+    def blocks(item, num):
+        rows, cols = own[item].shape
+        if item == SMALL:
+            return small.at[pl.ds(N0, num)]
+        if item in CHAN1:
+            return w1.at[CHAN1.index(item), pl.ds(N0, num * rows), pl.ds(N0, cols)]
+        if item in CHAN2:
+            return w2.at[CHAN2.index(item), pl.ds(N0, num * rows), pl.ds(N0, cols)]
+        return (stem_w if item == STEM_W else head_w).at[pl.ds(N0, num * rows), pl.ds(N0, cols)]
+
+    def arrivals(item, num, slot):
+        view = blocks(item, num)
+        pltpu.make_async_remote_copy(src_ref=view, dst_ref=view, send_sem=send_sem.at[item],
+                                     recv_sem=recv_sem.at[item, slot], device_id=device_of(coords, core),
+                                     device_id_type=MESH).wait_recv()
+
     def move(item, part, bits, is_own, target, slot):
         lo, num = GATHER_SPLITS[item][part]
         there = block(item, *owner_of(shifted(coords, bits), core), lo, num)
         here = own[item].at[pl.ds(lo, num), :] if is_own else there
-        pltpu.make_async_remote_copy(src_ref=here, dst_ref=there, send_sem=send_sem,
-                                     recv_sem=recv_sem.at[item, part, slot], device_id=target,
+        pltpu.make_async_remote_copy(src_ref=here, dst_ref=there, send_sem=send_sem.at[item],
+                                     recv_sem=recv_sem.at[item, slot], device_id=target,
                                      device_id_type=MESH).start()
 
-    def arrival(item, part, bits, from_core, slot):
-        lo, num = GATHER_SPLITS[item][part]
-        there = block(item, *owner_of(shifted(coords, bits), from_core), lo, num)
-        pltpu.make_async_remote_copy(src_ref=there, dst_ref=there, send_sem=send_sem,
-                                     recv_sem=recv_sem.at[item, part, slot], device_id=device_of(coords, core),
-                                     device_id_type=MESH).wait_recv()
-
     def pass_on(item, part, bits, level):
-        order = ORDERS[part]
-        rank = sum(N2 ** i for i in DIMS if bits[order[i]])
         for step in range(level, N3):
-            move(item, part, bits, False, device_of(shifted(coords, unit(order[step])), core), N2 ** step - N1 + rank)
-        move(item, part, bits, False, device_of(coords, N1 - core), N7 + rank)
+            move(item, part, bits, False, device_of(shifted(coords, unit(ORDERS[part][step])), core), step)
+        move(item, part, bits, False, device_of(coords, N1 - core), N3)
 
     def bits_of(part, rank):
         bits = [N0, N0, N0]
@@ -241,21 +252,18 @@
         for step in DIMS:
             for part in DIMS:
                 target = device_of(shifted(coords, unit(ORDERS[part][step])), core)
-                move(item, part, none, True, target, N2 ** step - N1)
+                move(item, part, none, True, target, step)
         for part in DIMS:
-            move(item, part, none, True, device_of(coords, N1 - core), N7)
+            move(item, part, none, True, device_of(coords, N1 - core), N3)
 
     def forward(item, level):
-        for part in DIMS:
-            for rank in range(N2 ** level):
-                bits = bits_of(part, rank + N2 ** level)
-                arrival(item, part, bits, core, N2 ** level - N1 + rank)
-                pass_on(item, part, bits, level + N1)
+        arrivals(item, N2 ** level, level)
+        for rank in range(N2 ** level):
+            for part in DIMS:
+                pass_on(item, part, bits_of(part, rank + N2 ** level), level + N1)
 
     def finish(item):
-        for part in DIMS:
-            for rank in range(N8):
-                arrival(item, part, bits_of(part, rank), N1 - core, N7 + rank)
+        arrivals(item, N8, N3)
 
     def place_own(item):
         here = own[item]
@@ -417,7 +425,9 @@
     row_max = jnp.maximum(*[jnp.max(jnp.where(real, l, -jnp.inf), axis=N1, keepdims=True) for l in logits])
     exps = [jnp.where(real, jnp.exp(jnp.where(real, l, row_max) - row_max), 0.0) for l in logits]
     sums = jnp.sum(exps[N0], axis=N1, keepdims=True) + jnp.sum(exps[N1], axis=N1, keepdims=True)
-    mine = labels[pl.ds(aligned(tp * IMAGES, N8), IMAGES), :]
+    square = (IMAGES, labels.shape[N1])
+    chosen = lax.broadcasted_iota(jnp.int32, square, N1) == lax.broadcasted_iota(jnp.int32, square, N0) + tp * IMAGES
+    mine = jnp.sum(jnp.where(chosen, labels[...].astype(F32), 0.0), axis=N1, keepdims=True).astype(jnp.int32)
     hits = [jnp.logical_and(lane + z * CLASSES_HALF == mine, real) for z in range(N2)]
     picked = sum(jnp.sum(jnp.where(hit, l, 0.0), axis=N1, keepdims=True) for hit, l in zip(hits, logits))
     losses = row_max + jnp.log(sums) - picked
@@ -440,14 +450,12 @@
 
     for k, (src, dst) in enumerate(saves):
         pltpu.make_async_copy(src, dst, save_sem.at[k]).wait()
-    for item in range(GATHERED):
-        for part in DIMS:
-            lo, num = GATHER_SPLITS[item][part]
-            here = own[item].at[pl.ds(lo, num), :]
-            for _ in range(15):
-                pltpu.make_async_remote_copy(src_ref=here, dst_ref=here, send_sem=send_sem,
-                                             recv_sem=recv_sem.at[item, part, N0], device_id=device_of(coords, core),
-                                             device_id_type=MESH).wait_send()
+    whole = [stem_w, small, w1.at[N0], w2.at[N0], w1.at[N1], w2.at[N1], head_w]
+    for item, ref in enumerate(whole):
+        view = ref.at[pl.ds(N0, ref.shape[N0] // 16 * 15)]
+        pltpu.make_async_remote_copy(src_ref=view, dst_ref=view, send_sem=send_sem.at[item],
+                                     recv_sem=recv_sem.at[item, N0], device_id=device_of(coords, core),
+                                     device_id_type=MESH).wait_send()
 
 
 def forward_all(*operands):
@@ -472,7 +480,7 @@
             pltpu.VMEM((N2, TOK, 256), BF16)] + [pltpu.VMEM(blocks, F32)] * N5 + [
             pltpu.VMEM(plane, BF16), pltpu.VMEM(plane, F32), pltpu.VMEM(plane, BF16),
             pltpu.VMEM((IMAGES, WIDE), F32),
-            dma, dma((GATHERED, N3, 15)), dma, dma((N8,))],
+            dma((GATHERED,)), dma((GATHERED, N4)), dma, dma((N8,))],
         compiler_params=pltpu.CompilerParams(collective_id=N0, has_side_effects=True, vmem_limit_bytes=67043328),
         cost_estimate=pl.CostEstimate(flops=10 ** 9, bytes_accessed=25 * 10 ** N6, transcendentals=N0),
         name='forward')(*operands)
@@ -499,7 +507,7 @@
     send_sem, hop_sem, peer_sem, pair_sem, load_sem, red_send, red_recv = grab(N7)
     coords, core = my_position()
     other = N1 - core
-    entry_barrier(coords, core)
+    barrier_signal(coords, core)
     partner = device_of(coords, other)
     pending = []
 
@@ -591,6 +599,12 @@
         return gh_hbm.at[pl.ds(aligned(f * 64, 64), 64), :]
     first = [load(w1_hbm.at[N1], w1, N0), load(w2_hbm.at[N1], w2, N1), load(xb_hbm.at[N1], xb, N2)]
     xa_copy = load(xa_hbm.at[N1], xa, N4)
+    osum[...] = hs[...]
+
+    @pl.loop(N0, TOK)
+    def _(t):
+        put(grad, pl.ds(aligned(t * IMAGES, IMAGES), IMAGES), d0[...])
+    barrier_wait()
     heads = []
     for y in range(N2):
         for x in range(N2):
@@ -600,11 +614,6 @@
                                      peer[HEAD].at[z, y, x], pair_sem.at[slot], partner))
                 heads.append(load(head_view(y * N4 + x * N2 + core).at[:, pl.ds(z * WIDE, WIDE)],
                                   mine[HEAD].at[z, y, x], N5 + slot))
-    osum[...] = hs[...]
-
-    @pl.loop(N0, TOK)
-    def _(t):
-        put(grad, pl.ds(aligned(t * IMAGES, IMAGES), IMAGES), d0[...])
 
     def head_start():
         for y in range(N2):
@@ -732,28 +741,27 @@
     final = [(otok.at[N0], tbox.at[N0], N0), (osum, sbox, N2)]
     layer1, layer0 = (CH1[N1], CH2[N1]), (CH1[N0], CH2[N0])
 
+    def nothing():
+        pass
+
     for copy in first:
         copy.wait()
-    channel_back(N1, [head_start, lambda: advance([HEAD], N0), lambda: advance([HEAD], N1),
-                     lambda: advance([HEAD], N2, [oh])])
+    channel_back(N1, [head_start, nothing, lambda: advance([HEAD], N0), lambda: advance([HEAD], N1)])
     again = [load(w1_hbm.at[N0], w1, N0), load(w2_hbm.at[N0], w2, N1), load(xb_hbm.at[N0], xb, N2)]
     xa_copy.wait()
-    token_back(N1, [(N5, lambda: advance(layer1, N0))])
+    token_back(N1, [(N1, lambda: advance([HEAD], N2, [oh])), (N7, lambda: advance(layer1, N0))])
     reduce_send(late, N0)
     xa_copy = load(xa_hbm.at[N0], xa, N4)
     for copy in again:
         copy.wait()
 
-    def second():
+    def last():
         advance(layer1, N1)
         reduce_step(late, N1)
-
-    def third():
-        advance(layer1, N2, [o1.at[N1], o2.at[N1]])
-        reduce_step(late, N2)
-    channel_back(N0, [lambda: reduce_step(late, N0), second, third, lambda: reduce_step(late, N3)])
+    channel_back(N0, [nothing, lambda: reduce_step(late, N0), nothing, last])
     xa_copy.wait()
-    token_back(N0, [(N5, lambda: advance(layer0, N0))])
+    token_back(N0, [(N2, lambda: advance(layer1, N2, [o1.at[N1], o2.at[N1]])), (N3, lambda: reduce_step(late, N2)),
+                   (N7, lambda: advance(layer0, N0))])
 
     @pl.loop(N0, STRIPS)
     def _(i):
@@ -790,19 +798,19 @@
         if k == N3:
             stem_left()
             reduce_step(final, N0)
-        if k == N5:
-            advance(layer0, N1)
     for k in range(N4):
         for z in range(N2):
             arrived(peer[STEM].at[z, k // N2, k % N2], pair_sem.at[N2 * k + z])
     add_peer(STEM)
     phase_send(STEM, N0)
+    reduce_step(late, N3)
     reduce_step(final, N1)
+    advance(layer0, N1)
+    advance([STEM], N0)
+    reduce_step(final, N2)
     advance(layer0, N2, [o1.at[N0], o2.at[N0]])
-    reduce_step(final, N2)
-    advance([STEM], N0)
+    advance([STEM], N1)
     reduce_step(final, N3)
-    advance([STEM], N1)
     advance([STEM], N2, [o_stem])
     for copy in pending:
         copy.wait_send()
@@ -895,7 +903,7 @@
             return values.reshape(N1, -N1)
         by_token = patches.swapaxes(N0, N1)
         w1, w2, xa, xb, t1t, t1, t2, bt, vec, gh, hs, d0 = forward_all(
-            by_token, labels.reshape(-N1, N1), w_stem, w_ch1, w_ch2, w_head, flat(b_stem), ln1_g, ln1_b, ln2_g, ln2_b,
+            by_token, flat(labels), w_stem, w_ch1, w_ch2, w_head, flat(b_stem), ln1_g, ln1_b, ln2_g, ln2_b,
             b_ch2, flat(lnf_g), flat(lnf_b), b_ch1, b_tok1, flat(b_head), w_tok1.swapaxes(N1, N2), w_tok2)
         sums = backward_all(w1, w2, t1t, t1, t2, bt, vec, xa, xb, d0, by_token, gh, hs)
         (loss, g_stem, g_ch1, g_ch2, g_head, gb_stem, g1_g, g1_b, g2_g, g2_b, gb_ch2, gf_g, gf_b,

time: 234 us -> 216 us (0.923)
  Pallas kernels: 231 us -> 215 us
    pallas_call x1, Pallas kernels: 147 us -> 134 us  [backward_all(): pl.pallas_call(backward_kernel, out_shape=[jax.ShapeDtypeStruct(s, F32) f...]
    pallas_call x1, Pallas kernels: 80.8 us -> 78.2 us  [forward_all(): pl.pallas_call(forward_kernel, out_shape=outs, in_specs=[any_spec] + [vme...]
where the time goes in v4:
time: 216 us; the launch traced here: 215 us
  Pallas kernels  215 us (100%)
    pallas_call x1, Pallas kernels, backward_all(): pl.pallas_call(backward_kernel, out_shape=[jax.ShapeDtypeStruct(s, F32) f...  134 us
    pallas_call x1, Pallas kernels, forward_all(): pl.pallas_call(forward_kernel, out_shape=outs, in_specs=[any_spec] + [vme...  78.2 us

profile of v4, /device:TPU:0, one launch (start us, length us, event | category | flops | bytes accessed | tf_op | source)
XLA Modules:
  0.0 215.5 jit_solution(13773660889675132701)
XLA Ops:
  0.7 78.2 %forward.1 = (bf16[2,512,2048]{2,1,0:T(8,128)(2,1)}, bf16[2,2048,512]{2,1,0:T(8,128)(2,1)}, f32[2,4,784,128]{3,2,1,0:T(8,128)}, f32[2,4,784,128]{3,2,1,0:T(8,128...) custom-call(bf16[49,32,3072]{2,1,0:T(8,128)(2,1)} %bitcast.13, ...), custom_call_target="tpu_custom_call" | custom-call | flops 1000000000 | bytes 25000000 | tf_op jit(solution)/shard_map/forward/pallas_call | solution.py:471
  78.8 133.6 %backward.1 = (f32[256,384]{1,0:T(8,128)}, f32[2,64,1024]{2,1,0:T(8,128)}, f32[2,512,128]{2,1,0:T(8,128)}, f32[64,512]{1,0:T(8,128)}, f32[24,512]{1,0:T(8,128)}, /*index=5*/f32[2,256,128]{2,1,0:T(8,128)}) custom-call(bf16[2,512,2048]{2,1,0:T(8,128)(2,1)} %get-tuple-element.54.refs_0_, bf16[2,2048,512]{2,1,0:T(8,128)(2,1)} %get-tuple-element.55.refs_1_, ...), custom_call_target="tpu_custom_call" | custom-call | flops 1000000000 | bytes 50000000 | tf_op jit(solution)/shard_map/backward/pallas_call | solution.py:832
  212.4 2.9 %finish.1 = (f32[1,1]{1,0:T(1,128)}, f32[384,256]{1,0:T(8,128)}, f32[2,64,1024]{2,1,0:T(8,128)}, f32[2,128,512]{2,1,0:T(8,128)}, f32[64,500]{1,0:T(8,128)}, /*in...) custom-call(f32[256,384]{1,0:T(8,128)} %get-tuple-element.66.refs_0_, ...), custom_call_target="tpu_custom_call" | custom-call | tf_op jit(solution)/shard_map/finish/pallas_call | solution.py:887
